TPU v7x, 128 devices: a whole 4x4x4 slice. The times are simulated.
128 devices in a mesh: dom: 32 (over x, y, core), shift: 4 (over z).
Axes of the slice: x: 4, y: 4, z: 4, core: 2. Of those that a mesh axis runs over, the one named last changes fastest.
Arguments:
- sources: float32 [32, 128, 16, 128], P('shift', 'dom'), may hold values from -6 to 6
- kappa: float32 [128, 16, 128], P('dom'), may hold values from 0 to 2
- mass: float32 [128, 16, 128], P('dom'), may hold values from 0.25 to 4
- shift_table: float32 [64], replicated, may hold values from 0.5 to 4
- shift_ids: int32 [16], P('shift'), may hold values from 0 to 63
- sketch: bfloat16 [1024, 128, 16, 128], P(None, 'dom'), may hold values from -0.1875 to 0.1875
Outputs:
- solution: float32 [16, 32, 128, 16, 128], P('shift', None, 'dom')
- residual: float32 [16, 32, 128, 16, 128], P('shift', None, 'dom')
Inputs may be any that keep to these rules, and one draw needn't show every extreme that they name: `shift_ids`: index into shift_table.
All inputs are finite; a program needn't handle non-finite values.
Results may differ from a plain program's by a relative error of at most 0.0026.
Values sent between devices are 32-bit elements; how exact they have to be, the bound alone decides.
A program may use at most 128 MiB of HBM per device.

v0:
```python
import functools

import jax
import jax.numpy as jnp
from jax import lax
from jax.experimental import pallas as pl
from jax.experimental.pallas import tpu as pltpu
from jax.sharding import PartitionSpec as P

HALO = 3
PIECES = 2
LANES = 128
MID = 2.25
BASIS = 10
IMAGES = ((1, 2), (3, 4, 5), (6, 7, 8, 9))
PAIRS = [(i, k) for i in range(BASIS) for k in range(i, BASIS)]
PAIR_INDEX = {pair: n for n, pair in enumerate(PAIRS)}


def neighbour_sum(field):
    inner = field[1:-1]
    shape = inner.shape
    total = field[2:] + field[:-2]
    for dim in (1, 2):
        size = shape[dim]
        place = lax.broadcasted_iota(jnp.int32, shape, dim)
        total = total + jnp.where(place > 0, pltpu.roll(inner, 1, dim), 0.0)
        total = total + jnp.where(place < size - 1, pltpu.roll(inner, size - 1, dim), 0.0)
    return total


def plane_mask(shape, width, low, high):
    plane = lax.broadcasted_iota(jnp.int32, shape, 0)
    return jnp.where(plane < width, low, jnp.where(plane >= shape[0] - width, high, 1.0))


def edge_flags():
    me = lax.axis_index("dom")
    last = lax.axis_size("dom") - 1
    return (me > 0).astype(jnp.float32), (me < last).astype(jnp.float32)


def basis_fields(w0, diag, mass, mask1, mask2):
    sixth = 1.0 / 6.0
    center = 6.0 + MID
    d1, m1 = diag[1:-1], mass[1:-1]
    d2, m2 = diag[2:-2], mass[2:-2]
    d3, m3 = diag[3:-3], mass[3:-3]
    w0i = w0[1:-1]
    a0 = d1 * w0i - neighbour_sum(w0)
    a1 = m1 * w0i
    scaled1 = sixth * mask1
    g0 = (a0 - center * w0i) * scaled1
    g1 = (a1 - w0i) * scaled1
    g0i, g1i = g0[1:-1], g1[1:-1]
    b0 = d2 * g0i - neighbour_sum(g0)
    b1 = d2 * g1i - neighbour_sum(g1) + m2 * g0i
    b2 = m2 * g1i
    scaled2 = sixth * mask2
    h0 = (b0 - center * g0i) * scaled2
    h1 = (b1 - center * g1i - g0i) * scaled2
    h2 = (b2 - g1i) * scaled2
    h0i, h1i, h2i = h0[1:-1], h1[1:-1], h2[1:-1]
    e0 = d3 * h0i - neighbour_sum(h0)
    e1 = d3 * h1i - neighbour_sum(h1) + m3 * h0i
    e2 = d3 * h2i - neighbour_sum(h2) + m3 * h1i
    e3 = m3 * h2i
    return [
        w0[3:-3], a0[2:-2], a1[2:-2], b0[1:-1], b1[1:-1], b2[1:-1], e0, e1, e2, e3
    ]


def solve_small(h_vals, entry):
    l00 = jnp.sqrt(entry[0][0])
    l10 = entry[1][0] / l00
    l20 = entry[2][0] / l00
    l11 = jnp.sqrt(entry[1][1] - l10 * l10)
    l21 = (entry[2][1] - l20 * l10) / l11
    l22 = jnp.sqrt(entry[2][2] - l20 * l20 - l21 * l21)
    f0 = h_vals[0] / l00
    f1 = (h_vals[1] - l10 * f0) / l11
    f2 = (h_vals[2] - l20 * f0 - l21 * f1) / l22
    c2 = f2 / l22
    c1 = (f1 - l21 * c2) / l11
    c0 = (f0 - l10 * c1 - l20 * c2) / l00
    return (c0, c1, c2)


def coefficients(gram, tau):
    def product(left, right):
        by_degree = {}
        for p, i in enumerate(left):
            for q, k in enumerate(right):
                n = PAIR_INDEX[(min(i, k), max(i, k))]
                column = gram[:, n : n + 1]
                by_degree[p + q] = by_degree[p + q] + column if p + q in by_degree else column
        top = max(by_degree)
        total = jnp.broadcast_to(by_degree[top], (gram.shape[0], LANES))
        for degree in range(top - 1, -1, -1):
            total = total * tau + by_degree[degree]
        return total

    h_vals = [product(image, (0,)) for image in IMAGES]
    entry = [[None] * 3 for _ in range(3)]
    for i in range(3):
        for k in range(i + 1):
            entry[i][k] = product(IMAGES[i], IMAGES[k])
    ridge = 0.001 * (entry[0][0] + entry[1][1] + entry[2][2]) / 3.0 + 1.0
    for i in range(3):
        entry[i][i] = entry[i][i] + ridge
    return solve_small(h_vals, entry)


def project_kernel(
    n, groups, src_hbm, kappa_hbm, mass_hbm, table_ref, ids_ref, sketch_ref,
    wide_ref, coeff_ref, c_ref,
    src_ref, kappa_ref, mass_ref, mine_ref, rows_buf, raw_ref, fields_ref, out_buf, in_buf, gram_own, gram_in, gram_all,
    load_sem, in_sem, own_sem, own_send, own_recv, z_send, z_recv, halo_send, halo_recv, km_send, km_recv,
    rs_send, rs_recv, g_send, g_recv, s_send, s_recv,
):
    me = lax.axis_index("dom")
    group = lax.axis_index("shift")
    nb, slab = src_ref.shape[0], src_ref.shape[1]
    block = rows_buf.shape[1]
    columns = BASIS * nb
    right, left = lax.rem(me + 1, n), lax.rem(me + n - 1, n)
    has_right, has_left = me < n - 1, me > 0

    def remote(src, dst, send, recv, **where):
        return pltpu.make_async_remote_copy(
            src_ref=src, dst_ref=dst, send_sem=send, recv_sem=recv,
            device_id=where, device_id_type=pl.DeviceIdType.MESH,
        )

    def load(t):
        owner = lax.rem(me + 1 + t, n)
        return pltpu.make_async_copy(
            sketch_ref.at[pl.ds(owner * block, block)], rows_buf.at[t], load_sem.at[t]
        )

    barrier = pltpu.get_barrier_semaphore()
    for t in range(1, n):
        pl.semaphore_signal(
            barrier, inc=1, device_id={"dom": lax.rem(me + t, n)},
            device_id_type=pl.DeviceIdType.MESH,
        )
    for t in range(1, groups):
        pl.semaphore_signal(
            barrier, inc=1, device_id={"shift": lax.rem(group + t, groups)},
            device_id_type=pl.DeviceIdType.MESH,
        )
    arguments = [
        pltpu.make_async_copy(src_hbm, src_ref, in_sem.at[0]),
        pltpu.make_async_copy(kappa_hbm, kappa_ref, in_sem.at[1]),
        pltpu.make_async_copy(mass_hbm, mass_ref, in_sem.at[2]),
    ]
    for copy in arguments:
        copy.start()
    for t in range(n):
        load(t).start()
    for copy in arguments:
        copy.wait()
    pl.semaphore_wait(barrier, n - 1 + groups - 1)

    def sides(side):
        if side == 0:
            return slab - HALO, pl.ds(0, HALO), right
        return 0, pl.ds(slab + HALO, HALO), left

    def own_halo(side):
        first, target, there = sides(side)
        return remote(
            src_ref.at[:, pl.ds(first, HALO)], mine_ref.at[:, target],
            own_send.at[side], own_recv.at[side], dom=there,
        )

    hops = []
    for k in range(1, groups // 2 + 1):
        for way in range(2):
            parts = (0, nb)
            if 2 * k == groups:
                parts = ((0, nb // 2), (nb // 2, nb - nb // 2))[way]
            hops.append((way, k, pl.ds(*parts)))

    def shifted(way, k):
        step = k if way == 0 else groups - k
        return lax.rem(group + step, groups)

    def across(hop):
        way, k, part = hop
        if k == 1:
            slot, src = group, src_ref.at[part]
        else:
            slot = shifted(1 - way, k - 1)
            src = wide_ref.at[slot, part, pl.ds(HALO, slab)]
        return remote(
            src, wide_ref.at[slot, part, pl.ds(HALO, slab)],
            z_send.at[way, k - 1], z_recv.at[way, k - 1], shift=shifted(way, 1),
        )

    def halo(hop, side):
        way, k, part = hop
        slot = shifted(1 - way, k)
        first, target, there = sides(side)
        return remote(
            wide_ref.at[slot, part, pl.ds(HALO + first, HALO)], wide_ref.at[slot, part, target],
            halo_send.at[way, k - 1, side], halo_recv.at[way, k - 1, side], dom=there,
        )

    def coeff_halo(which, side):
        ref = (kappa_ref, mass_ref)[which]
        first, target, there = sides(side)
        return remote(
            ref.at[pl.ds(first, HALO)], coeff_ref.at[which, target], km_send.at[which, side],
            km_recv.at[which, side], dom=there,
        )

    @pl.when(has_right)
    def _():
        own_halo(0).start()
        for which in range(2):
            coeff_halo(which, 0).start()

    @pl.when(has_left)
    def _():
        own_halo(1).start()
        for which in range(2):
            coeff_halo(which, 1).start()

    for hop in hops:
        if hop[1] == 1:
            across(hop).start()

    mine_ref[:, pl.ds(HALO, slab)] = src_ref[...]
    coeff_ref[0, pl.ds(HALO, slab)] = kappa_ref[...]
    coeff_ref[1, pl.ds(HALO, slab)] = mass_ref[...]

    @pl.when(jnp.logical_not(has_left))
    def _():
        mine_ref[:, pl.ds(0, HALO)] = jnp.zeros(
            (nb, HALO) + src_ref.shape[2:], jnp.float32
        )
        coeff_ref[:, pl.ds(0, HALO)] = jnp.zeros((2, HALO) + src_ref.shape[2:], jnp.float32)

    @pl.when(jnp.logical_not(has_right))
    def _():
        mine_ref[:, pl.ds(slab + HALO, HALO)] = jnp.zeros(
            (nb, HALO) + src_ref.shape[2:], jnp.float32
        )
        coeff_ref[:, pl.ds(slab + HALO, HALO)] = jnp.zeros(
            (2, HALO) + src_ref.shape[2:], jnp.float32
        )

    @pl.when(has_left)
    def _():
        own_halo(0).wait_recv()
        for which in range(2):
            coeff_halo(which, 0).wait_recv()

    @pl.when(has_right)
    def _():
        own_halo(1).wait_recv()
        for which in range(2):
            coeff_halo(which, 1).wait_recv()

    keep = pltpu.make_async_copy(mine_ref, wide_ref.at[group], own_sem)
    keep.start()
    low, high = edge_flags()
    mass = coeff_ref[1]
    diag = (6.0 - coeff_ref[0]) + MID * mass
    planes = slab + 2 * HALO
    grid_tail = src_ref.shape[2:]
    mask1 = plane_mask((planes - 2,) + grid_tail, 2, low, high)
    mask2 = plane_mask((planes - 4,) + grid_tail, 1, low, high)

    def one_source(b, carry):
        fields = basis_fields(mine_ref[b], diag, mass, mask1, mask2)
        for k, field in enumerate(fields):
            rounded = field.astype(jnp.bfloat16)
            raw_ref[k * nb + b] = rounded
            raw_ref[columns + k * nb + b] = (field - rounded.astype(jnp.float32)).astype(
                jnp.bfloat16
            )
        return carry

    lax.fori_loop(0, nb, one_source, 0)
    fields_ref[...] = raw_ref[...].reshape(fields_ref.shape)

    def forward(hop):
        across(hop).wait_recv()
        for later in hops:
            if later[0] == hop[0] and later[1] == hop[1] + 1:
                across(later).start()

        @pl.when(has_right)
        def _():
            halo(hop, 0).start()

        @pl.when(has_left)
        def _():
            halo(hop, 1).start()

    early = [hop for hop in hops if hop[1] < groups // 2]
    late = [hop for hop in hops if hop[1] == groups // 2]
    def scatter(t):
        return remote(
            out_buf.at[t], in_buf.at[t], rs_send.at[t], rs_recv.at[t],
            dom=lax.rem(me + 1 + t, n),
        )

    per = next(size for size in (PIECES, 2, 1) if n % size == 0)

    def multiply(u):
        for t in range(per):
            load(u * per + t).wait()
        product = lax.dot_general(
            rows_buf[pl.ds(u * per, per)].reshape(per * block, fields_ref.shape[1]),
            fields_ref[...], (((1,), (1,)), ((), ())), preferred_element_type=jnp.float32,
        )
        turned = product.T
        summed = turned[:columns] + turned[columns:]
        return [summed[:, t * block : (t + 1) * block] for t in range(per)]

    def send(t, piece):
        out_buf[t] = piece
        scatter(t).start()

    def step(u, carry):
        for t, piece in enumerate(multiply(u)):
            send(u * per + t, piece)
        return carry

    lax.fori_loop(0, n // per - 1, step, 0)
    pieces = multiply(n // per - 1)
    for t in range(per - 1):
        send(n - per + t, pieces[t])
    total = pieces[per - 1]
    for hop in early:
        forward(hop)

    for t in range(n - 1):
        scatter(t).wait_recv()
        total = total + in_buf[t]

    lane = lax.broadcasted_iota(jnp.int32, (nb, LANES), 1)
    gram = jnp.zeros((nb, LANES), jnp.float32)
    for p, (i, k) in enumerate(PAIRS):
        value = jnp.sum(
            total[i * nb : (i + 1) * nb] * total[k * nb : (k + 1) * nb], axis=1, keepdims=True
        )
        gram = jnp.where(lane == p, value, gram)
    gram_own[...] = gram

    def share(t):
        return remote(
            gram_own, gram_in.at[t - 1], g_send.at[t - 1], g_recv.at[t - 1],
            dom=lax.rem(me + t, n),
        )

    for t in range(1, n):
        share(t).start()
    for t in range(1, n):
        share(t).wait_recv()
        gram = gram + gram_in[t - 1]
    gram_all[group] = gram
    for hop in late:
        forward(hop)

    def spread(t):
        return remote(
            gram_all.at[group], gram_all.at[group], s_send.at[t - 1], s_recv.at[t - 1],
            shift=lax.rem(group + t, groups),
        )

    for t in range(1, groups):
        spread(t).start()
    tau = jnp.zeros((1, LANES), jnp.float32)
    lane_row = lax.broadcasted_iota(jnp.int32, (1, LANES), 1)
    for j in range(ids_ref.shape[0]):
        tau = jnp.where(lane_row == j, table_ref[ids_ref[j]] - MID, tau)
    for t in range(1, groups):
        spread(t).wait_recv()
    count = groups * nb
    solved = coefficients(gram_all[...].reshape(count, LANES), tau)
    shifts = ids_ref.shape[0]
    packed = jnp.zeros((count, LANES), jnp.float32)
    lane_count = lax.broadcasted_iota(jnp.int32, (count, LANES), 1)
    for i in range(3):
        value = jnp.where(lane_count < shifts, solved[i], 0.0)
        packed = packed + (pltpu.roll(value, i * shifts, 1) if i else value)
    c_ref[...] = packed

    for hop in hops:
        @pl.when(has_left)
        def _():
            halo(hop, 0).wait_recv()

        @pl.when(has_right)
        def _():
            halo(hop, 1).wait_recv()

    keep.wait()

    @pl.when(has_right)
    def _():
        own_halo(0).wait_send()
        for hop in hops:
            halo(hop, 0).wait_send()
        for which in range(2):
            coeff_halo(which, 0).wait_send()

    @pl.when(has_left)
    def _():
        own_halo(1).wait_send()
        for hop in hops:
            halo(hop, 1).wait_send()
        for which in range(2):
            coeff_halo(which, 1).wait_send()

    for t in range(1, groups):
        spread(t).wait_send()
    for hop in hops:
        across(hop).wait_send()
    for t in range(n - 1):
        scatter(t).wait_send()
    for t in range(1, n):
        share(t).wait_send()


def combine_kernel(wide_ref, coeff_ref, c_ref, table_ref, ids_ref, sol_ref, res_ref, step_ref):
    batch, planes = wide_ref.shape[0], wide_ref.shape[1]
    me = lax.axis_index("dom")
    has_low, has_high = me > 0, me < lax.axis_size("dom") - 1
    shifts = ids_ref.shape[0]
    first = pl.program_id(0) * batch

    def inside(field, width):
        return jnp.concatenate(
            [
                jnp.where(has_low, field[:width], 0.0),
                field[width:-width],
                jnp.where(has_high, field[-width:], 0.0),
            ],
            axis=0,
        )

    @pl.when(pl.program_id(0) == 0)
    def _():
        for j in range(shifts):
            sigma = table_ref[ids_ref[j]]
            step_ref[j] = sigma * (coeff_ref[1, 1:-1] - 1.0) - coeff_ref[0, 1:-1]

    def one_source(i, carry):
        w0 = inside(wide_ref[i], HALO)
        own = w0[3:-3]
        near = neighbour_sum(w0)
        b = first + i
        for j in range(shifts):
            center = 6.0 + table_ref[ids_ref[j]]
            v1 = inside(step_ref[j] * w0[1:-1] - near, 2)
            v2 = inside(step_ref[j, 1:-1] * v1[1:-1] - neighbour_sum(v1), 1)
            v3 = step_ref[j, 2:-2] * v2[1:-1] - neighbour_sum(v2)
            v1, v2 = v1[2:-2], v2[1:-1]
            c0 = c_ref[b, j]
            c1 = c_ref[b, shifts + j] * (1.0 / 6.0)
            c2 = c_ref[b, 2 * shifts + j] * (1.0 / 36.0)
            sol_ref[j, i] = c0 * own + c1 * v1 + c2 * v2
            res_ref[j, i] = (
                (1.0 - c0 * center) * own - (c0 + c1 * center) * v1
                - (c1 + c2 * center) * v2 - c2 * v3
            )
        return carry

    lax.fori_loop(0, batch, one_source, 0)


def on_device(sources, kappa, mass, shift_table, shift_ids, sketch):
    n, groups = lax.axis_size("dom"), lax.axis_size("shift")
    nb, slab = sources.shape[0], sources.shape[1]
    tail = sources.shape[2:]
    shifts = shift_ids.shape[0]
    rows = sketch.shape[0]
    block = rows // n
    cells = slab * tail[0] * tail[1]
    planes = slab + 2 * HALO
    count = groups * nb
    columns = BASIS * nb
    vmem = pl.BlockSpec(memory_space=pltpu.VMEM)
    hbm = pl.BlockSpec(memory_space=pl.ANY)
    smem = pl.BlockSpec(memory_space=pltpu.SMEM)
    dma = pltpu.SemaphoreType.DMA
    f32 = jnp.float32
    wide, coeff, solved = pl.pallas_call(
        functools.partial(project_kernel, n, groups),
        out_shape=(
            jax.ShapeDtypeStruct((groups, nb, planes) + tail, f32),
            jax.ShapeDtypeStruct((2, planes) + tail, f32),
            jax.ShapeDtypeStruct((count, LANES), f32),
        ),
        in_specs=[hbm, hbm, hbm, smem, smem, hbm],
        out_specs=(hbm, vmem, vmem),
        scratch_shapes=[
            pltpu.VMEM(sources.shape, f32),
            pltpu.VMEM(kappa.shape, f32),
            pltpu.VMEM(mass.shape, f32),
            pltpu.VMEM((nb, planes) + tail, f32),
            pltpu.VMEM((n, block, slab) + tail, jnp.bfloat16),
            pltpu.VMEM((2 * columns, slab) + tail, jnp.bfloat16),
            pltpu.VMEM((2 * columns, cells), jnp.bfloat16),
            pltpu.VMEM((n - 1, columns, block), f32),
            pltpu.VMEM((n - 1, columns, block), f32),
            pltpu.VMEM((nb, LANES), f32),
            pltpu.VMEM((n - 1, nb, LANES), f32),
            pltpu.VMEM((groups, nb, LANES), f32),
            dma((n,)),
            dma((3,)), dma,
            dma((2,)), dma((2,)),
            dma((2, groups // 2)), dma((2, groups // 2)),
            dma((2, groups // 2, 2)), dma((2, groups // 2, 2)),
            dma((2, 2)), dma((2, 2)),
            dma((n - 1,)), dma((n - 1,)),
            dma((n - 1,)), dma((n - 1,)),
            dma((groups - 1,)), dma((groups - 1,)),
        ],
        compiler_params=pltpu.CompilerParams(
            collective_id=0, has_side_effects=True, vmem_limit_bytes=56 << 20
        ),
        name="project",
    )(sources, kappa, mass, shift_table, shift_ids, sketch)

    batch = 4 if count % 4 == 0 else 1
    out = jax.ShapeDtypeStruct((shifts, count, slab) + tail, f32)
    out_spec = pl.BlockSpec((shifts, batch, slab) + tail, lambda i: (0, i, 0, 0, 0))
    return pl.pallas_call(
        combine_kernel,
        grid=(count // batch,),
        out_shape=(out, out),
        in_specs=[
            pl.BlockSpec((batch, planes) + tail, lambda i: (i, 0, 0, 0)),
            pl.BlockSpec((2, planes) + tail, lambda i: (0, 0, 0, 0)),
            smem, smem, smem,
        ],
        out_specs=(out_spec, out_spec),
        scratch_shapes=[pltpu.VMEM((shifts, planes - 2) + tail, f32)],
        compiler_params=pltpu.CompilerParams(vmem_limit_bytes=63 << 20),
        name="combine",
    )(wide.reshape((count, planes) + tail), coeff, solved, shift_table, shift_ids)


def solution(mesh):
    placed = (
        P("shift", "dom", None, None),
        P("dom", None, None),
        P("dom", None, None),
        P(),
        P("shift"),
        P(None, "dom", None, None),
    )
    return jax.shard_map(
        on_device,
        mesh=mesh,
        in_specs=placed,
        out_specs=(P("shift", None, "dom", None, None), P("shift", None, "dom", None, None)),
        check_vma=False,
    )
```

profile of v0, /device:TPU:1, one launch (start us, length us, event | category | flops | bytes accessed | tf_op | source)
XLA Modules:
  0.0 74.8 jit_solution(17447269455269235985)
XLA Ops:
  0.6 59.2 %project.1 = (f32[4,8,10,16,128]{4,3,2,1,0:T(8,128)}, f32[2,10,16,128]{3,2,1,0:T(8,128)}, f32[32,128]{1,0:T(8,128)}) custom-call(f32[8,4,16,128]{3,2,1,0:T(8,128)} %src_hbm.1, f32[4,16,128]{2,1,0:T(8,128)} %kappa_hbm.1, f32[4,16,128]{2,1,0:T(8,128)} %mass_hbm.1, f32[64]{0:T(128)} %table_ref.3, s32[4]{0:T(128)} %ids_ref.3, bf16[1024,4,16,128]{3,2,1,0:T(8,128)(2,1)} %sketch_ref.1), custom_call_target="tpu_custom_call" | custom-call | tf_op jit(solution)/shard_map/project/pallas_call | solution.py:493
  59.9 14.9 %combine.1 = (f32[4,32,4,16,128]{4,3,2,1,0:T(8,128)}, f32[4,32,4,16,128]{4,3,2,1,0:T(8,128)}) custom-call(f32[32,10,16,128]{3,2,1,0:T(8,128)} %bitcast.1, f32[2,10,16,128]{3,2,1,0:T(8,128)} %get-tuple-element.6.coeff_ref, f32[32,128]{1,0:T(8,128)} %get-tuple-element.7.c_ref, f32[64]{0:T(128)} %table_ref.3, s32[4]{0:T(128)} %ids_ref.3), custom_call_target="tpu_custom_call" | custom-call | tf_op jit(solution)/shard_map/combine/pallas_call | solution.py:534
where the time goes:
time: 74.9 us; the launch traced here: 74.8 us
  Pallas kernels  74.1 us (99%)
    pallas_call x1, Pallas kernels, on_device(): pl.pallas_call(functools.partial(project_kernel, n, groups), out_shape=(j...  59.2 us
    pallas_call x1, Pallas kernels, on_device(): pl.pallas_call(combine_kernel, grid=(count // batch,), out_shape=(out, ou...  14.9 us

commit v1 on v0

v1 whole, which is shorter than its diff:
```python
import functools

import jax
import jax.numpy as jnp
from jax import lax
from jax.experimental import pallas as pl
from jax.experimental.pallas import tpu as pltpu
from jax.sharding import PartitionSpec as P

HALO = 3
LANES = 128
MID = 2.25
F32 = jnp.float32
BF16 = jnp.bfloat16
BASIS = 10
SPLIT = 6
IMAGES = ((0,), (1, 6), (2, 3, 7), (4, 5, 8, 9))
VMEM_SPEC = pl.BlockSpec(memory_space=pltpu.VMEM)
HBM_SPEC = pl.BlockSpec(memory_space=pltpu.HBM)
SMEM_SPEC = pl.BlockSpec(memory_space=pltpu.SMEM)
DMA = pltpu.SemaphoreType.DMA


def in_hbm(array):
    return pltpu.with_memory_space_constraint(array, pltpu.HBM)


def in_vmem(array):
    return pltpu.with_memory_space_constraint(array, pltpu.VMEM)


def remote(src, dst, send, recv, **where):
    return pltpu.make_async_remote_copy(
        src_ref=src, dst_ref=dst, send_sem=send, recv_sem=recv,
        device_id=where, device_id_type=pl.DeviceIdType.MESH,
    )


def signal(sem, **where):
    pl.semaphore_signal(sem, inc=1, device_id=where, device_id_type=pl.DeviceIdType.MESH)


def plane_of(ref, p, ny):
    return ref[pl.ds(p * ny, ny)]


def neighbour_sum(ref, p, ny):
    inner = plane_of(ref, p, ny)
    total = plane_of(ref, p - 1, ny) + plane_of(ref, p + 1, ny)
    none = jnp.zeros((1,) + inner.shape[1:], F32)
    total = total + jnp.concatenate([none, inner[:-1]], axis=0)
    total = total + jnp.concatenate([inner[1:], none], axis=0)
    lane = lax.broadcasted_iota(jnp.int32, inner.shape, 2)
    total = total + jnp.where(lane > 0, pltpu.roll(inner, 1, 2), 0.0)
    return total + jnp.where(lane < LANES - 1, pltpu.roll(inner, LANES - 1, 2), 0.0)


def edge_flag(p, planes, width, low, high):
    if p < width:
        return low
    return high if p >= planes - width else None


def masked(value, flag):
    return value if flag is None else value * flag


def edge_flags(me, n):
    return (me > 0).astype(F32), (me < n - 1).astype(F32)


def prepare_kernel(
    n, ny, src_hbm, kappa_hbm, mass_hbm, sketch_hbm,
    sketch_out, weights_out, wide_out, kappa_out, mass1,
    wide, kappa, mass, diag, g0, g1, h0, h1, h2,
    load_sem, in_sem, halo_send, halo_recv,
):
    me = lax.axis_index("dom")
    nb, rows = src_hbm.shape[0], src_hbm.shape[1]
    slab = rows // ny
    right, left = lax.rem(me + 1, n), lax.rem(me + n - 1, n)
    has_right, has_left = me < n - 1, me > 0
    depth = HALO * ny
    thin = (HALO - 1) * ny

    barrier = pltpu.get_barrier_semaphore()

    @pl.when(has_right)
    def _():
        signal(barrier, dom=right)

    @pl.when(has_left)
    def _():
        signal(barrier, dom=left)

    inputs = [
        pltpu.make_async_copy(src_hbm.at[b], wide.at[pl.ds(depth, rows), b], in_sem.at[b])
        for b in range(nb)
    ]
    inputs.append(pltpu.make_async_copy(kappa_hbm, kappa.at[pl.ds(thin, rows)], in_sem.at[nb]))
    inputs.append(pltpu.make_async_copy(mass_hbm, mass.at[pl.ds(thin, rows)], in_sem.at[nb + 1]))
    for copy in inputs:
        copy.start()

    def load(k):
        return pltpu.make_async_copy(sketch_hbm.at[:, k], sketch_out.at[k], load_sem.at[k])

    loads = sketch_hbm.shape[1]
    early = 4
    for k in range(early):
        load(k).start()
    for copy in inputs:
        copy.wait()

    def halo(which, side):
        ref, width = ((wide, depth), (kappa, thin), (mass, thin))[which]
        first, target, there = ((rows, 0, right), (width, width + rows, left))[side]
        return remote(
            ref.at[pl.ds(first, width)], ref.at[pl.ds(target, width)],
            halo_send.at[which, side], halo_recv.at[which, side], dom=there,
        )

    pl.semaphore_wait(barrier, has_right.astype(jnp.int32) + has_left.astype(jnp.int32))

    @pl.when(has_right)
    def _():
        for which in range(3):
            halo(which, 0).start()

    @pl.when(has_left)
    def _():
        for which in range(3):
            halo(which, 1).start()

    for k in range(early, loads):
        load(k).start()

    @pl.when(jnp.logical_not(has_left))
    def _():
        wide.reshape(wide.shape[0], nb, LANES)[pl.ds(0, depth)] = jnp.zeros((depth, nb, LANES), F32)
        kappa[pl.ds(0, thin)] = jnp.zeros((thin, 1, LANES), F32)
        mass[pl.ds(0, thin)] = jnp.zeros((thin, 1, LANES), F32)

    @pl.when(jnp.logical_not(has_right))
    def _():
        wide.reshape(wide.shape[0], nb, LANES)[pl.ds(depth + rows, depth)] = jnp.zeros(
            (depth, nb, LANES), F32
        )
        kappa[pl.ds(thin + rows, thin)] = jnp.zeros((thin, 1, LANES), F32)
        mass[pl.ds(thin + rows, thin)] = jnp.zeros((thin, 1, LANES), F32)

    @pl.when(has_left)
    def _():
        for which in range(3):
            halo(which, 0).wait_recv()

    @pl.when(has_right)
    def _():
        for which in range(3):
            halo(which, 1).wait_recv()

    full = (ny, nb, LANES)
    field = wide.reshape(wide.shape[0], nb, LANES)
    low, high = edge_flags(me, n)
    planes = slab + 2 * HALO
    for p in range(planes - 2):
        k = jnp.broadcast_to(kappa[pl.ds(p * ny, ny)], full)
        m = jnp.broadcast_to(mass[pl.ds(p * ny, ny)] - 1.0, full)
        diag[pl.ds(p * ny, ny)] = MID * m - k
        mass1[pl.ds(p * ny, ny)] = m
        kappa_out[pl.ds(p * ny, ny)] = k
    for p in range(planes):
        wide_out[pl.ds(p * ny, ny)] = plane_of(field, p, ny)

    for p in range(planes - 2):
        flag = edge_flag(p, planes - 2, 2, low, high)
        w = plane_of(field, p + 1, ny)
        out = pl.ds(p * ny, ny)
        g0[out] = masked(diag[out] * w - neighbour_sum(field, p + 1, ny), flag)
        g1[out] = mass1[out] * w
    for p in range(planes - 4):
        flag = edge_flag(p, planes - 4, 1, low, high)
        at, out = pl.ds((p + 1) * ny, ny), pl.ds(p * ny, ny)
        d, m = diag[at], mass1[at]
        u0, u1 = g0[at], g1[at]
        h0[out] = masked(d * u0 - neighbour_sum(g0, p + 1, ny), flag)
        h1[out] = masked(d * u1 - neighbour_sum(g1, p + 1, ny) + m * u0, flag)
        h2[out] = m * u1
    for p in range(slab):
        at, inner = pl.ds((p + 2) * ny, ny), pl.ds((p + 1) * ny, ny)
        d, m = diag[at], mass1[at]
        v0, v1, v2 = h0[inner], h1[inner], h2[inner]
        e0 = d * v0 - neighbour_sum(h0, p + 1, ny)
        e1 = d * v1 - neighbour_sum(h1, p + 1, ny) + m * v0
        e2 = d * v2 - neighbour_sum(h2, p + 1, ny) + m * v1
        e3 = m * v2
        first = jnp.concatenate(
            [plane_of(field, p + HALO, ny), g0[at], v0, v1, e0, e1], axis=1
        )
        second = jnp.concatenate([g1[at], v2, e2, e3], axis=1)
        high_part = first.astype(BF16)
        low_part = (first - high_part.astype(F32)).astype(BF16)
        columns = jnp.concatenate([high_part, second.astype(BF16), low_part], axis=1)
        pairs = ny // 2
        weights_out[pl.ds(p * pairs, pairs)] = columns.reshape(pairs, 2 * columns.shape[1], LANES)

    for k in range(loads):
        load(k).wait()

    @pl.when(has_right)
    def _():
        for which in range(3):
            halo(which, 0).wait_send()

    @pl.when(has_left)
    def _():
        for which in range(3):
            halo(which, 1).wait_send()


def solve_small(h_vals, entry):
    l00 = jnp.sqrt(entry[0][0])
    l10 = entry[1][0] / l00
    l20 = entry[2][0] / l00
    l11 = jnp.sqrt(entry[1][1] - l10 * l10)
    l21 = (entry[2][1] - l20 * l10) / l11
    l22 = jnp.sqrt(entry[2][2] - l20 * l20 - l21 * l21)
    f0 = h_vals[0] / l00
    f1 = (h_vals[1] - l10 * f0) / l11
    f2 = (h_vals[2] - l20 * f0 - l21 * f1) / l22
    c2 = f2 / l22
    c1 = (f1 - l21 * c2) / l11
    c0 = (f0 - l10 * c1 - l20 * c2) / l00
    return (c0, c1, c2)


def pair_lane(i, k):
    distance = (k - i) % BASIS
    if distance <= BASIS // 2:
        return BASIS * distance + i
    return BASIS * (BASIS - distance) + k


def coefficients(gram, sigma):
    tau, center = sigma - MID, sigma + 6.0

    def product(left, right):
        by_degree = {}
        for p, i in enumerate(IMAGES[left]):
            for q, k in enumerate(IMAGES[right]):
                at = pair_lane(i, k)
                column = gram[:, at : at + 1]
                by_degree[p + q] = by_degree[p + q] + column if p + q in by_degree else column
        top = max(by_degree)
        total = jnp.broadcast_to(by_degree[top], gram.shape)
        for degree in range(top - 1, -1, -1):
            total = total * tau + by_degree[degree]
        return total

    ww = [[product(i, k) if i <= k else None for k in range(4)] for i in range(4)]

    def between(i, k):
        total = ww[i][k]
        if i > 0:
            total = total + center * ww[i - 1][k]
        if k > 0:
            low = ww[min(i, k - 1)][max(i, k - 1)]
            if i > 0:
                low = low + center * ww[i - 1][k - 1]
            total = total + center * low
        return total

    scale = (1.0, 1.0, 1.0 / 6.0, 1.0 / 36.0)
    h_vals = [between(0, i) * scale[i] for i in (1, 2, 3)]
    entry = [[None] * 3 for _ in range(3)]
    for i in range(3):
        for k in range(i + 1):
            entry[i][k] = between(k + 1, i + 1) * (scale[i + 1] * scale[k + 1])
    ridge = 0.001 * (entry[0][0] + entry[1][1] + entry[2][2]) / 3.0 + 1.0
    for i in range(3):
        entry[i][i] = entry[i][i] + ridge
    c0, c1, c2 = solve_small(h_vals, entry)
    c1, c2 = c1 * (1.0 / 6.0), c2 * (1.0 / 36.0)
    return (c0, c1, c2, 1.0 - c0 * center, c0 + c1 * center, c1 + c2 * center)


def project_kernel(
    n, groups, ny, sketch_ref, weights_ref, own_ref, kappa_ref, mass1_ref, table_ref, ids_ref,
    fields_out, own_out, coeff_out,
    wide, step_ref, product, picked, near, first, second, out_buf, in_buf, rows_buf,
    z_send, z_recv, halo_send, halo_recv, rs_send, rs_recv, g_send, g_recv, s_send, s_recv,
):
    me = lax.axis_index("dom")
    group = lax.axis_index("shift")
    planes = own_ref.shape[0] // ny
    nb = own_ref.shape[1]
    slab = planes - 2 * HALO
    rows, depth = slab * ny, HALO * ny
    right, left = lax.rem(me + 1, n), lax.rem(me + n - 1, n)
    has_right, has_left = me < n - 1, me > 0
    shifts = ids_ref.shape[0]
    low, high = edge_flags(me, n)

    barrier = pltpu.get_barrier_semaphore()
    for t in range(1, n):
        signal(barrier, dom=lax.rem(me + t, n))
    for t in range(1, groups):
        signal(barrier, shift=lax.rem(group + t, groups))

    hops = []
    for k in range(1, groups // 2 + 1):
        for way in range(2):
            part = (0, slab)
            if 2 * k == groups:
                part = ((0, slab // 2), (slab // 2, slab - slab // 2))[way]
            hops.append((way, k, part))

    def shifted(way, k):
        return lax.rem(group + (k if way == 0 else groups - k), groups)

    def across(hop):
        way, k, (start, count) = hop
        at = pl.ds(depth + start * ny, count * ny)
        slot = group if k == 1 else shifted(1 - way, k - 1)
        src = own_ref.at[at] if k == 1 else wide.at[slot, at]
        return remote(
            src, wide.at[slot, at], z_send.at[way, k - 1], z_recv.at[way, k - 1],
            shift=shifted(way, 1),
        )

    def arrived(hop):
        way, k, _ = hop
        return shifted(1 - way, k)

    def halo(index, slot, side):
        start, target, there = ((rows, 0, right), (depth, depth + rows, left))[side]
        return remote(
            wide.at[slot, pl.ds(start, depth)], wide.at[slot, pl.ds(target, depth)],
            halo_send.at[index, side], halo_recv.at[index, side], dom=there,
        )

    def slot_of(index):
        if index == 2:
            return shifted(0, 2)
        return shifted(1 - index, 1)

    def send_halo(index):
        slot = slot_of(index)

        @pl.when(has_right)
        def _():
            halo(index, slot, 0).start()

        @pl.when(has_left)
        def _():
            halo(index, slot, 1).start()

    def take_halo(index):
        slot = slot_of(index)

        @pl.when(has_left)
        def _():
            halo(index, slot, 0).wait_recv()

        @pl.when(has_right)
        def _():
            halo(index, slot, 1).wait_recv()

        @pl.when(jnp.logical_not(has_left))
        def _():
            wide[slot, pl.ds(0, depth)] = jnp.zeros((depth, nb, LANES), F32)

        @pl.when(jnp.logical_not(has_right))
        def _():
            wide[slot, pl.ds(depth + rows, depth)] = jnp.zeros((depth, nb, LANES), F32)

    per = 2
    steps = sketch_ref.shape[0] // per

    def multiply(u):
        at = [u * per + i for i in range(per)]
        return lax.dot_general(
            jnp.concatenate([sketch_ref[k] for k in at], axis=1),
            jnp.concatenate([weights_ref[k] for k in at], axis=1),
            (((1,), (1,)), ((), ())), preferred_element_type=F32,
        )

    def accumulate(u, carry):
        product[...] += multiply(u)
        return carry

    product[...] = multiply(0)
    lax.fori_loop(1, steps // 2, accumulate, 0)
    pl.semaphore_wait(barrier, n - 1 + groups - 1)
    for hop in hops:
        if hop[1] == 1:
            across(hop).start()
    lax.fori_loop(steps // 2, steps, accumulate, 0)

    half = product.shape[1] // 2
    odd = lax.rem(lax.broadcasted_iota(jnp.int32, picked.shape, 0), 2) == 1
    picked[...] = jnp.where(odd, product[:, half:], product[:, :half])
    count = picked.shape[0] // 2
    turned = (picked[pl.ds(0, count, stride=2)] + picked[pl.ds(1, count, stride=2)]).T
    split, columns = SPLIT * nb, BASIS * nb
    sketched = jnp.concatenate([turned[:split] + turned[columns:], turned[split:columns]], axis=0)
    chunks = count // LANES
    flat_out = out_buf.reshape(chunks * columns, LANES)
    for r in range(chunks):
        flat_out[pl.ds(r * columns, columns)] = sketched[:, r * LANES : (r + 1) * LANES]
    parts = n // nb
    span = chunks // parts

    def piece(dest):
        return out_buf.at[pl.ds(dest // nb * span, span), :, lax.rem(dest, nb)]

    def scatter(t):
        dest = lax.rem(me + t, n)
        return remote(
            piece(dest), in_buf.at[me, :, pl.ds(0, BASIS)], rs_send.at[t - 1], rs_recv.at[t - 1],
            dom=dest,
        )

    for t in range(1, n):
        scatter(t).start()
    in_buf[me, :, pl.ds(0, BASIS)] = piece(me)[...]

    for hop in hops:
        if hop[1] == 1:
            across(hop).wait_recv()
    for hop in hops:
        if hop[1] == 2:
            across(hop).start()
    for index in range(2):
        send_halo(index)

    def images(field, slot):
        for p in range(planes - 2):
            near[pl.ds(p * ny, ny)] = neighbour_sum(field, p + 1, ny)

        def one_shift(j, carry):
            for p in range(planes - 2):
                at = pl.ds(p * ny, ny)
                flag = edge_flag(p, planes - 2, 2, low, high)
                first[at] = masked(step_ref[j, at] * plane_of(field, p + 1, ny) - near[at], flag)
            for p in range(planes - 4):
                at = pl.ds((p + 1) * ny, ny)
                flag = edge_flag(p, planes - 4, 1, low, high)
                second[pl.ds(p * ny, ny)] = masked(
                    step_ref[j, at] * first[at] - neighbour_sum(first, p + 1, ny), flag
                )
            for p in range(slab):
                at, inner, out = pl.ds((p + 2) * ny, ny), pl.ds((p + 1) * ny, ny), pl.ds(p * ny, ny)
                fields_out[slot, j, 0, out] = first[at]
                fields_out[slot, j, 1, out] = second[inner]
                fields_out[slot, j, 2, out] = (
                    step_ref[j, at] * second[inner] - neighbour_sum(second, p + 1, ny)
                )
            return carry

        lax.fori_loop(0, shifts, one_shift, 0)
        for p in range(slab):
            own_out[slot, pl.ds(p * ny, ny)] = plane_of(field, p + HALO, ny)

    for j in range(shifts):
        step_ref[j] = table_ref[ids_ref[j]] * mass1_ref[...] - kappa_ref[...]
    images(own_ref, group)

    flat_in = in_buf.reshape(n * span * in_buf.shape[2], LANES)
    tall = span * in_buf.shape[2]
    for t in range(1, n):
        scatter(t).wait_recv()
    total = flat_in[pl.ds(0, tall)]
    for t in range(1, n):
        total = total + flat_in[pl.ds(t * tall, tall)]
    lane = lax.broadcasted_iota(jnp.int32, (BASIS, LANES), 1)
    place = lax.broadcasted_iota(jnp.int32, (BASIS, LANES), 0)
    views = [total[r * in_buf.shape[2] :][:BASIS] for r in range(span)]
    twice = [jnp.concatenate([view, view], axis=0) for view in views]
    packed = jnp.zeros((BASIS, LANES), F32)
    for d in range(BASIS // 2 + 1):
        terms = sum(view * wrap[d : d + BASIS] for view, wrap in zip(views, twice))
        packed = jnp.where(lane == place + BASIS * d, jnp.sum(terms, axis=1, keepdims=True), packed)
    rows_buf[group, me] = jnp.sum(packed, axis=0, keepdims=True)

    def share(t):
        return remote(
            rows_buf.at[group, me], rows_buf.at[group, me], g_send.at[t - 1], g_recv.at[t - 1],
            dom=lax.rem(me + t, n),
        )

    for t in range(1, n):
        share(t).start()
    for hop in hops:
        if hop[1] == 2:
            across(hop).wait_recv()
    send_halo(2)
    take_halo(0)
    images(wide.at[slot_of(0)], slot_of(0))
    take_halo(1)
    images(wide.at[slot_of(1)], slot_of(1))
    for t in range(1, n):
        share(t).wait_recv()

    def spread(t):
        return remote(
            rows_buf.at[group], rows_buf.at[group], s_send.at[t - 1], s_recv.at[t - 1],
            shift=lax.rem(group + t, groups),
        )

    for t in range(1, groups):
        spread(t).start()
    take_halo(2)
    images(wide.at[slot_of(2)], slot_of(2))
    for t in range(1, groups):
        spread(t).wait_recv()

    lane_row = lax.broadcasted_iota(jnp.int32, (1, LANES), 1)
    sigma = jnp.full((1, LANES), MID, F32)
    for j in range(shifts):
        sigma = jnp.where(lane_row == j, table_ref[ids_ref[j]], sigma)
    flat_rows = rows_buf.reshape(groups * n, LANES)
    gram = []
    for g in range(groups):
        block = flat_rows[pl.ds(g * n, n)]
        gram.append(sum(block[q * nb : (q + 1) * nb] for q in range(parts)))
    solved = coefficients(jnp.concatenate(gram, axis=0), sigma)
    for i, value in enumerate(solved):
        for j in range(shifts):
            spreaded = jnp.broadcast_to(value[:, j : j + 1], value.shape)
            coeff_out[j, i] = spreaded.reshape(groups, nb, LANES)

    for index in range(3):
        slot = slot_of(index)

        @pl.when(has_right)
        def _():
            halo(index, slot, 0).wait_send()

        @pl.when(has_left)
        def _():
            halo(index, slot, 1).wait_send()

    for hop in hops:
        across(hop).wait_send()
    for t in range(1, n):
        scatter(t).wait_send()
        share(t).wait_send()
    for t in range(1, groups):
        spread(t).wait_send()


def combine_kernel(fields_ref, own_ref, coeff_ref, sol_hbm, res_hbm, sol_buf, res_buf, sem):
    groups, shifts = fields_ref.shape[0], fields_ref.shape[1]
    rows, nb = fields_ref.shape[3], fields_ref.shape[4]

    def copies(g, j):
        out = []
        for which, (buf, hbm) in enumerate(((sol_buf, sol_hbm), (res_buf, res_hbm))):
            for b in range(nb):
                out.append(
                    pltpu.make_async_copy(
                        buf.at[g, j, :, b], hbm.at[j, g * nb + b], sem.at[which, g, j, b]
                    )
                )
        return out

    def one(u, carry):
        g, j = u // shifts, lax.rem(u, shifts)
        c = [coeff_ref[j, i, g][None] for i in range(6)]
        w0 = own_ref[g]
        w1, w2, w3 = (fields_ref[g, j, i] for i in range(3))
        sol_buf.at[g, j].reshape(rows, nb, LANES)[...] = c[0] * w0 + c[1] * w1 + c[2] * w2
        res_buf.at[g, j].reshape(rows, nb, LANES)[...] = (
            c[3] * w0 - c[4] * w1 - c[5] * w2 - c[2] * w3
        )
        for copy in copies(g, j):
            copy.start()
        return carry

    lax.fori_loop(0, groups * shifts, one, 0)

    def finish(u, carry):
        for copy in copies(u // shifts, lax.rem(u, shifts)):
            copy.wait()
        return carry

    lax.fori_loop(0, groups * shifts, finish, 0)


def on_device(sources, kappa, mass, shift_table, shift_ids, sketch):
    n, groups = lax.axis_size("dom"), lax.axis_size("shift")
    nb, slab, ny = sources.shape[0], sources.shape[1], sources.shape[2]
    shifts = shift_ids.shape[0]
    sk = sketch.shape[0]
    rows = slab * ny
    planes = slab + 2 * HALO
    wide_rows, inner = planes * ny, (planes - 2) * ny
    pairs = rows // 2
    weights = 2 * (BASIS + SPLIT) * nb
    vec = (nb, LANES)
    sketch, weight, wide, kappa, mass = pl.pallas_call(
        functools.partial(prepare_kernel, n, ny),
        out_shape=(
            pltpu.VMEM((pairs, sk, 2, LANES), BF16),
            pltpu.VMEM((pairs, weights, LANES), BF16),
            pltpu.VMEM((wide_rows,) + vec, F32),
            pltpu.VMEM((inner,) + vec, F32),
            pltpu.VMEM((inner,) + vec, F32),
        ),
        in_specs=[HBM_SPEC] * 4,
        out_specs=(VMEM_SPEC,) * 5,
        scratch_shapes=[
            pltpu.VMEM((wide_rows, nb, 1, LANES), F32),
            pltpu.VMEM((inner, 1, LANES), F32),
            pltpu.VMEM((inner, 1, LANES), F32),
            pltpu.VMEM((inner,) + vec, F32),
            pltpu.VMEM((inner,) + vec, F32),
            pltpu.VMEM((inner,) + vec, F32),
            pltpu.VMEM((inner - 2 * ny,) + vec, F32),
            pltpu.VMEM((inner - 2 * ny,) + vec, F32),
            pltpu.VMEM((inner - 2 * ny,) + vec, F32),
            DMA((pairs,)), DMA((nb + 2,)), DMA((3, 2)), DMA((3, 2)),
        ],
        compiler_params=pltpu.CompilerParams(
            collective_id=0, has_side_effects=True, vmem_limit_bytes=16 << 20
        ),
        name="prepare",
    )(
        in_hbm(sources.reshape(nb, rows, 1, LANES)), in_hbm(kappa.reshape(rows, 1, LANES)),
        in_hbm(mass.reshape(rows, 1, LANES)), in_hbm(sketch.reshape(sk, pairs, 2, LANES)),
    )
    parts = n // nb
    span = sk // LANES // parts
    fields, own, coeff = pl.pallas_call(
        functools.partial(project_kernel, n, groups, ny),
        out_shape=(
            pltpu.VMEM((groups, shifts, 3, rows) + vec, F32),
            pltpu.VMEM((groups, rows) + vec, F32),
            pltpu.VMEM((shifts, 6, groups) + vec, F32),
        ),
        in_specs=[VMEM_SPEC] * 5 + [SMEM_SPEC] * 2,
        out_specs=(VMEM_SPEC,) * 3,
        scratch_shapes=[
            pltpu.VMEM((groups, wide_rows) + vec, F32),
            pltpu.VMEM((shifts, inner) + vec, F32),
            pltpu.VMEM((2 * sk, weights), F32),
            pltpu.VMEM((2 * sk, weights // 2), F32),
            pltpu.VMEM((inner,) + vec, F32),
            pltpu.VMEM((inner,) + vec, F32),
            pltpu.VMEM((inner - 2 * ny,) + vec, F32),
            pltpu.VMEM((sk // LANES, BASIS, nb, 1, LANES), F32),
            pltpu.VMEM((n, span, 16, 1, LANES), F32),
            pltpu.VMEM((groups, n, 1, LANES), F32),
            DMA((2, groups // 2)), DMA((2, groups // 2)),
            DMA((3, 2)), DMA((3, 2)),
            DMA((n - 1,)), DMA((n - 1,)),
            DMA((n - 1,)), DMA((n - 1,)),
            DMA((groups - 1,)), DMA((groups - 1,)),
        ],
        compiler_params=pltpu.CompilerParams(
            collective_id=1, has_side_effects=True, vmem_limit_bytes=16 << 20
        ),
        name="project",
    )(
        in_vmem(sketch.reshape(pairs, 2 * sk, LANES)), in_vmem(weight), in_vmem(wide), in_vmem(kappa),
        in_vmem(mass), shift_table, shift_ids,
    )

    out = pltpu.HBM((shifts, groups * nb, rows, 1, LANES), F32)
    buf = pltpu.VMEM((groups, shifts, rows, nb, 1, LANES), F32)
    solution, residual = pl.pallas_call(
        combine_kernel,
        out_shape=(out, out),
        in_specs=[VMEM_SPEC] * 3,
        out_specs=(HBM_SPEC,) * 2,
        scratch_shapes=[buf, buf, DMA((2, groups, shifts, nb))],
        compiler_params=pltpu.CompilerParams(vmem_limit_bytes=16 << 20),
        name="combine",
    )(in_vmem(fields), in_vmem(own), in_vmem(coeff))
    shape = (shifts, groups * nb, slab, ny, LANES)
    return solution.reshape(shape), residual.reshape(shape)


def solution(mesh):
    placed = (
        P("shift", "dom", None, None),
        P("dom", None, None),
        P("dom", None, None),
        P(),
        P("shift"),
        P(None, "dom", None, None),
    )
    return jax.shard_map(
        on_device,
        mesh=mesh,
        in_specs=placed,
        out_specs=(P("shift", None, "dom", None, None), P("shift", None, "dom", None, None)),
        check_vma=False,
    )
```

time: 74.9 us -> 47.4 us (0.63)
  Pallas kernels: 74.1 us -> 46.6 us
    pallas_call x2 -> x3, Pallas kernels: 74.1 us -> 46.6 us  [the longest x1 31.3 us: on_device(): pl.pallas_call(functools.partial(project_kernel, n, groups, ny), out_shap...]
where the time goes in v1:
time: 47.4 us; the launch traced here: 47.3 us
  Pallas kernels  46.6 us (98%)
  between operations  0.68 us (1%)
    pallas_call x1, Pallas kernels, on_device(): pl.pallas_call(functools.partial(project_kernel, n, groups, ny), out_shap...  31.3 us
    pallas_call x1, Pallas kernels, on_device(): pl.pallas_call(functools.partial(prepare_kernel, n, ny), out_shape=(pltpu...  9.82 us
    pallas_call x1, Pallas kernels, on_device(): pl.pallas_call(combine_kernel, out_shape=(out, out), in_specs=[VMEM_SPEC]...  5.51 us

profile of v1, /device:TPU:1, one launch (start us, length us, event | category | flops | bytes accessed | tf_op | source)
XLA Modules:
  0.0 47.3 jit_solution(391971197364666643)
XLA Ops:
  0.6 0.0 copy-start.1
  0.6 0.0 copy-start
  0.7 9.8 %prepare.1 = (bf16[32,1024,2,128]{3,2,1,0:T(2,128)(2,1)S(1)}, bf16[32,256,128]{2,1,0:T(8,128)(2,1)S(1)}, f32[160,8,128]{2,1,0:T(8,128)S(1)}, f32[128,8,128]{2,1,0:T(8,128)S(1)}, f32[128,8,128]{2,1,0:T(8,128)S(1)}) custom-call(f32[8,64,1,128]{3,2,1,0:T(1,128)} %bitcast.9, f32[64,1,128]{2,1,0:T(1,128)} %bitcast.10, f32[64,1,128]{2,1,0:T(1,128)} %bitcast.11, ...), custom_call_target="tpu_custom_call" | custom-call | tf_op jit(solution)/shard_map/prepare/pallas_call | solution.py:602
  10.5 0.0 copy-done.1
  10.5 0.0 copy-done
  10.5 31.3 %project.1 = (f32[4,4,3,64,8,128]{5,4,3,2,1,0:T(8,128)S(1)}, f32[4,64,8,128]{3,2,1,0:T(8,128)S(1)}, f32[4,6,4,8,128]{4,3,2,1,0:T(8,128)S(1)}) custom-call(bf16[32,2048,128]{2,1,0:T(8,128)(2,1)S(1)} %bitcast.7, bf16[32,256,128]{2,1,0:T(8,128)(2,1)S(1)} %get-tuple-element.13.weights_ref, f32[160,8,128]{2,1,0:T(8,128)S(1)} %get-tuple-element.14.own_ref, ...), custom_call_target="tpu_custom_call" | custom-call | tf_op jit(solution)/shard_map/project/pallas_call | solution.py:635
  41.8 5.5 %combine.1 = (f32[4,32,64,1,128]{4,3,2,1,0:T(1,128)}, f32[4,32,64,1,128]{4,3,2,1,0:T(1,128)}) custom-call(f32[4,4,3,64,8,128]{5,4,3,2,1,0:T(8,128)S(1)} %get-tuple-element.17.fields_ref, f32[4,64,8,128]{3,2,1,0:T(8,128)S(1)} %get-tuple-element.18.own_ref, f32[4,6,4,8,128]{4,3,2,1,0:T(8,128)S(1)} %get-tuple-element.19.coeff_ref), custom_call_target="tpu_custom_call" | custom-call | tf_op jit(solution)/shard_map/combine/pallas_call | solution.py:672
Async XLA Ops:
  0.6 9.9 %copy-start.1 = (s32[4]{0:T(128)S(1)}, s32[4]{0:T(128)}, u32[]{:S(2)}) copy-start(s32[4]{0:T(128)} %ids_ref.1) | copy-start | bytes 52
  0.6 9.9 %copy-start = (f32[64]{0:T(128)S(1)}, f32[64]{0:T(128)}, u32[]{:S(2)}) copy-start(f32[64]{0:T(128)} %table_ref.1) | copy-start | bytes 772

commit v2 on v1

v2 whole, which is shorter than its diff:
```python
import functools

import jax
import jax.numpy as jnp
from jax import lax
from jax.experimental import pallas as pl
from jax.experimental.pallas import tpu as pltpu
from jax.sharding import PartitionSpec as P

HALO = 3
LANES = 128
MID = 2.25
F32 = jnp.float32
BF16 = jnp.bfloat16
BASIS = 10
SPLIT = 6
IMAGES = ((0,), (1, 6), (2, 3, 7), (4, 5, 8, 9))
VMEM_SPEC = pl.BlockSpec(memory_space=pltpu.VMEM)
HBM_SPEC = pl.BlockSpec(memory_space=pltpu.HBM)
SMEM_SPEC = pl.BlockSpec(memory_space=pltpu.SMEM)
DMA = pltpu.SemaphoreType.DMA


def in_hbm(array):
    return pltpu.with_memory_space_constraint(array, pltpu.HBM)


def in_vmem(array):
    return pltpu.with_memory_space_constraint(array, pltpu.VMEM)


def remote(src, dst, send, recv, **where):
    return pltpu.make_async_remote_copy(
        src_ref=src, dst_ref=dst, send_sem=send, recv_sem=recv,
        device_id=where, device_id_type=pl.DeviceIdType.MESH,
    )


def signal(sem, **where):
    pl.semaphore_signal(sem, inc=1, device_id=where, device_id_type=pl.DeviceIdType.MESH)


def wrapped(index, size):
    return jnp.where(index >= size, index - size, index)


def drain(ref, sem):
    pltpu.make_async_copy(ref, ref, sem).wait()


def plane_of(ref, p, ny):
    return ref[pl.ds(p * ny, ny)]


def neighbour_sum(ref, p, ny):
    inner = plane_of(ref, p, ny)
    total = plane_of(ref, p - 1, ny) + plane_of(ref, p + 1, ny)
    none = jnp.zeros((1,) + inner.shape[1:], F32)
    total = total + jnp.concatenate([none, inner[:-1]], axis=0)
    total = total + jnp.concatenate([inner[1:], none], axis=0)
    lane = lax.broadcasted_iota(jnp.int32, inner.shape, 2)
    total = total + jnp.where(lane > 0, pltpu.roll(inner, 1, 2), 0.0)
    return total + jnp.where(lane < LANES - 1, pltpu.roll(inner, LANES - 1, 2), 0.0)


def edge_flag(p, planes, width, low, high):
    if p < width:
        return low
    return high if p >= planes - width else None


def masked(value, flag):
    return value if flag is None else value * flag


def edge_flags(me, n):
    return (me > 0).astype(F32), (me < n - 1).astype(F32)


def prepare_kernel(
    n, groups, ny, src_hbm, kappa_hbm, mass_hbm, sketch_hbm,
    sketch_out, weights_out, wide, passed_out, kappa_out, mass1,
    coef, diag, g0, g1, h0, h1, h2,
    load_sem, in_sem, wide_send, wide_recv, coef_send, coef_recv, z_send, z_recv,
):
    me = lax.axis_index("dom")
    group = lax.axis_index("shift")
    nb, rows = src_hbm.shape[0], src_hbm.shape[1]
    slab = rows // ny
    right, left = wrapped(me + 1, n), wrapped(me + n - 1, n)
    up, down = wrapped(group + 1, groups), wrapped(group + groups - 1, groups)
    has_right, has_left = me < n - 1, me > 0
    depth = HALO * ny
    thin = (HALO - 1) * ny
    planes = slab + 2 * HALO

    barrier = pltpu.get_barrier_semaphore()
    inputs = [
        pltpu.make_async_copy(src_hbm.at[b], wide.at[pl.ds(depth, rows), b], in_sem.at[0])
        for b in range(nb)
    ]
    inputs.append(pltpu.make_async_copy(kappa_hbm, coef.at[0, pl.ds(thin, rows)], in_sem.at[1]))
    inputs.append(pltpu.make_async_copy(mass_hbm, coef.at[1, pl.ds(thin, rows)], in_sem.at[1]))
    for copy in inputs:
        copy.start()

    @pl.when(has_right)
    def _():
        signal(barrier, dom=right)

    @pl.when(has_left)
    def _():
        signal(barrier, dom=left)

    signal(barrier, shift=up)
    signal(barrier, shift=down)

    def load(k):
        return pltpu.make_async_copy(sketch_hbm.at[:, k], sketch_out.at[k], load_sem.at[0])

    loads = sketch_hbm.shape[1]
    early = 6
    for k in range(early):
        load(k).start()
    drain(wide.at[pl.ds(depth, rows)], in_sem.at[0])
    drain(coef.at[:, pl.ds(thin, rows)], in_sem.at[1])

    def wide_halo(k, side):
        first, target, there = (
            (depth + rows - (k + 1) * ny, depth - (k + 1) * ny, right),
            (depth + k * ny, depth + rows + k * ny, left),
        )[side]
        return remote(
            wide.at[pl.ds(first, ny)], wide.at[pl.ds(target, ny)],
            wide_send.at[side], wide_recv.at[k, side], dom=there,
        )

    def coef_halo(side):
        first, target, there = ((rows, 0, right), (thin, thin + rows, left))[side]
        return remote(
            coef.at[:, pl.ds(first, thin)], coef.at[:, pl.ds(target, thin)],
            coef_send.at[side], coef_recv.at[side], dom=there,
        )

    def pass_on(way):
        count = passed_out.shape[1]
        there = (up, down)[way]
        return remote(
            wide.at[pl.ds(depth + way * count, count)], passed_out.at[way],
            z_send.at[0], z_recv.at[way], shift=there,
        )

    pl.semaphore_wait(barrier, has_right.astype(jnp.int32) + has_left.astype(jnp.int32) + 2)

    def send_halo(side):
        wide_halo(0, side).start()
        coef_halo(side).start()
        for k in range(1, HALO):
            wide_halo(k, side).start()

    pl.when(has_right)(lambda: send_halo(0))
    pl.when(has_left)(lambda: send_halo(1))
    for way in range(2):
        pass_on(way).start()
    for k in range(early, loads):
        load(k).start()

    field = wide.reshape(wide.shape[0], nb, LANES)

    @pl.when(jnp.logical_not(has_left))
    def _():
        field[pl.ds(0, depth)] = jnp.zeros((depth, nb, LANES), F32)
        coef[:, pl.ds(0, thin)] = jnp.zeros((2, thin, 1, LANES), F32)

    @pl.when(jnp.logical_not(has_right))
    def _():
        field[pl.ds(depth + rows, depth)] = jnp.zeros((depth, nb, LANES), F32)
        coef[:, pl.ds(thin + rows, thin)] = jnp.zeros((2, thin, 1, LANES), F32)

    full = (ny, nb, LANES)
    low, high = edge_flags(me, n)

    def factors(p):
        at = pl.ds(p * ny, ny)
        k = jnp.broadcast_to(coef[0, at], full)
        m = jnp.broadcast_to(coef[1, at] - 1.0, full)
        diag[at] = MID * m - k
        mass1[at] = m
        kappa_out[at] = k

    def level1(p):
        flag = edge_flag(p, planes - 2, 2, low, high)
        w = plane_of(field, p + 1, ny)
        out = pl.ds(p * ny, ny)
        g0[out] = masked(diag[out] * w - neighbour_sum(field, p + 1, ny), flag)
        g1[out] = mass1[out] * w

    def level2(p):
        flag = edge_flag(p, planes - 4, 1, low, high)
        at, out = pl.ds((p + 1) * ny, ny), pl.ds(p * ny, ny)
        d, m = diag[at], mass1[at]
        u0, u1 = g0[at], g1[at]
        h0[out] = masked(d * u0 - neighbour_sum(g0, p + 1, ny), flag)
        h1[out] = masked(d * u1 - neighbour_sum(g1, p + 1, ny) + m * u0, flag)
        h2[out] = m * u1

    def level3(p):
        at, inner = pl.ds((p + 2) * ny, ny), pl.ds((p + 1) * ny, ny)
        d, m = diag[at], mass1[at]
        v0, v1, v2 = h0[inner], h1[inner], h2[inner]
        e0 = d * v0 - neighbour_sum(h0, p + 1, ny)
        e1 = d * v1 - neighbour_sum(h1, p + 1, ny) + m * v0
        e2 = d * v2 - neighbour_sum(h2, p + 1, ny) + m * v1
        e3 = m * v2
        first = jnp.concatenate(
            [plane_of(field, p + HALO, ny), g0[at], v0, v1, e0, e1], axis=1
        )
        second = jnp.concatenate([g1[at], v2, e2, e3], axis=1)
        high_part = first.astype(BF16)
        low_part = (first - high_part.astype(F32)).astype(BF16)
        columns = jnp.concatenate([high_part, second.astype(BF16), low_part], axis=1)
        pairs = ny // 2
        weights_out[pl.ds(p * pairs, pairs)] = columns.reshape(pairs, 2 * columns.shape[1], LANES)

    done = [set(), set(), set(), set()]

    def advance(reach):
        ready = set(range(HALO - reach, planes - HALO + reach))
        if reach != 1:
            coefs = range(2, planes - 4) if reach == 0 else (0, 1, planes - 4, planes - 3)
            for p in (coefs if reach in (0, 2) else ()):
                factors(p)
        usable = range(2, planes - 4) if reach < 2 else range(planes - 2)
        for p in range(planes - 2):
            if p not in done[1] and {p, p + 1, p + 2} <= ready and p in usable:
                level1(p)
                done[1].add(p)
        for p in range(planes - 4):
            if p not in done[2] and {p, p + 1, p + 2} <= done[1]:
                level2(p)
                done[2].add(p)
        for p in range(slab):
            if p not in done[3] and {p, p + 1, p + 2} <= done[2]:
                level3(p)
                done[3].add(p)

    advance(0)
    pl.when(has_left)(lambda: wide_halo(0, 0).wait_recv())
    pl.when(has_right)(lambda: wide_halo(0, 1).wait_recv())
    advance(1)

    def take(side):
        coef_halo(side).wait_recv()
        wide_halo(1, side).wait_recv()

    pl.when(has_left)(lambda: take(0))
    pl.when(has_right)(lambda: take(1))
    advance(2)
    pl.when(has_left)(lambda: wide_halo(2, 0).wait_recv())
    pl.when(has_right)(lambda: wide_halo(2, 1).wait_recv())
    advance(3)
    for way in range(2):
        pass_on(way).wait_recv()
    drain(sketch_out, load_sem.at[0])

    def sent(side):
        drain(wide.at[pl.ds(0, depth)], wide_send.at[side])
        drain(coef.at[:, pl.ds(0, thin)], coef_send.at[side])

    pl.when(has_right)(lambda: sent(0))
    pl.when(has_left)(lambda: sent(1))
    drain(wide.at[pl.ds(depth, rows)], z_send.at[0])


def solve_small(h_vals, entry):
    l00 = jnp.sqrt(entry[0][0])
    l10 = entry[1][0] / l00
    l20 = entry[2][0] / l00
    l11 = jnp.sqrt(entry[1][1] - l10 * l10)
    l21 = (entry[2][1] - l20 * l10) / l11
    l22 = jnp.sqrt(entry[2][2] - l20 * l20 - l21 * l21)
    f0 = h_vals[0] / l00
    f1 = (h_vals[1] - l10 * f0) / l11
    f2 = (h_vals[2] - l20 * f0 - l21 * f1) / l22
    c2 = f2 / l22
    c1 = (f1 - l21 * c2) / l11
    c0 = (f0 - l10 * c1 - l20 * c2) / l00
    return (c0, c1, c2)


def pair_lane(i, k):
    distance = (k - i) % BASIS
    if distance <= BASIS // 2:
        return BASIS * distance + i
    return BASIS * (BASIS - distance) + k


def coefficients(gram, sigma):
    tau, center = sigma - MID, sigma + 6.0

    def product(left, right):
        by_degree = {}
        for p, i in enumerate(IMAGES[left]):
            for q, k in enumerate(IMAGES[right]):
                at = pair_lane(i, k)
                column = gram[:, at : at + 1]
                by_degree[p + q] = by_degree[p + q] + column if p + q in by_degree else column
        top = max(by_degree)
        total = jnp.broadcast_to(by_degree[top], gram.shape)
        for degree in range(top - 1, -1, -1):
            total = total * tau + by_degree[degree]
        return total

    ww = [[product(i, k) if i <= k else None for k in range(4)] for i in range(4)]

    def between(i, k):
        total = ww[i][k]
        if i > 0:
            total = total + center * ww[i - 1][k]
        if k > 0:
            low = ww[min(i, k - 1)][max(i, k - 1)]
            if i > 0:
                low = low + center * ww[i - 1][k - 1]
            total = total + center * low
        return total

    scale = (1.0, 1.0, 1.0 / 6.0, 1.0 / 36.0)
    h_vals = [between(0, i) * scale[i] for i in (1, 2, 3)]
    entry = [[None] * 3 for _ in range(3)]
    for i in range(3):
        for k in range(i + 1):
            entry[i][k] = between(k + 1, i + 1) * (scale[i + 1] * scale[k + 1])
    ridge = 0.001 * (entry[0][0] + entry[1][1] + entry[2][2]) / 3.0 + 1.0
    for i in range(3):
        entry[i][i] = entry[i][i] + ridge
    c0, c1, c2 = solve_small(h_vals, entry)
    c1, c2 = c1 * (1.0 / 6.0), c2 * (1.0 / 36.0)
    return (c0, c1, c2, 1.0 - c0 * center, c0 + c1 * center, c1 + c2 * center)


def project_kernel(
    n, groups, ny, sketch_ref, weights_ref, own_ref, passed_ref, kappa_ref, mass1_ref, table_ref, ids_ref,
    fields_out, own_out, coeff_out,
    wide, step_ref, picked, near, first, second, out_buf, in_buf, rows_buf,
    z_send, z_recv, halo_send, halo_recv, rs_send, rs_recv, g_send, g_recv, s_send, s_recv,
):
    me = lax.axis_index("dom")
    group = lax.axis_index("shift")
    planes = own_ref.shape[0] // ny
    nb = own_ref.shape[1]
    slab = planes - 2 * HALO
    rows, depth = slab * ny, HALO * ny
    right, left = wrapped(me + 1, n), wrapped(me + n - 1, n)
    around = [group] + [wrapped(group + t, groups) for t in range(1, groups)]
    up, down = around[1], around[groups - 1]
    has_right, has_left = me < n - 1, me > 0
    shifts = ids_ref.shape[0]
    low, high = edge_flags(me, n)

    barrier = pltpu.get_barrier_semaphore()
    for t in range(1, n):
        signal(barrier, dom=wrapped(me + t, n))
    for t in range(1, groups):
        signal(barrier, shift=around[t])

    slots = (down, up, around[groups // 2])
    half = passed_ref.shape[1]

    def across(way):
        at = pl.ds(depth + (1 - way) * half, half)
        return remote(
            own_ref.at[at], wide.at[way, at], z_send.at[0], z_recv.at[way], shift=(up, down)[way]
        )

    def beyond(way):
        return remote(
            passed_ref.at[way], wide.at[2, pl.ds(depth + way * half, half)],
            z_send.at[0], z_recv.at[2], shift=(up, down)[way],
        )

    def halo(index, side, src, first_plane, count):
        target = ((first_plane - (slab - HALO)) * ny, depth + rows + first_plane * ny)[side]
        return remote(
            src, wide.at[index, pl.ds(target, count * ny)],
            halo_send.at[side], halo_recv.at[index, side], dom=(right, left)[side],
        )

    def planes_for(side):
        return range(slab - HALO, slab) if side == 0 else range(HALO)

    def early_halo(index, side):
        held = range(index * slab // 2, (index + 1) * slab // 2)
        mine = [p for p in planes_for(side) if p in held]
        at = pl.ds((mine[0] - held[0]) * ny, len(mine) * ny)
        return halo(index, side, passed_ref.at[index, at], mine[0], len(mine))

    def late_halo(index, side):
        held = range((1 - index) * slab // 2, (2 - index) * slab // 2)
        if index == 2:
            held = range(slab)
        mine = [p for p in planes_for(side) if p in held]
        at = pl.ds(depth + mine[0] * ny, len(mine) * ny)
        return halo(index, side, wide.at[index, at], mine[0], len(mine))

    def to_both(start):
        pl.when(has_right)(lambda: start(0))
        pl.when(has_left)(lambda: start(1))

    def take_halo(index):
        def take(side):
            drain(wide.at[index, pl.ds(0, depth)], halo_recv.at[index, side])

        pl.when(has_left)(lambda: take(0))
        pl.when(has_right)(lambda: take(1))

    steps = sketch_ref.shape[0] // 2
    tall = sketch_ref.shape[1] // 2

    def stage(u):
        tile = jnp.concatenate([weights_ref[2 * u], weights_ref[2 * u + 1]], axis=1)
        for unit in range(2):
            pltpu.matmul_push_rhs(tile, 0, unit, transpose=True)

    def multiply(accs):
        def accumulate(u):
            for unit in range(2):
                at = pl.ds(unit * tall, tall)
                part = jnp.concatenate([sketch_ref[2 * u, at], sketch_ref[2 * u + 1, at]], axis=1)
                pltpu.matmul_acc_lhs(accs[unit], part, load_staged_rhs=0)

        def step(u, carry):
            accumulate(u)
            stage(u + 1)
            return carry

        for acc in accs:
            pltpu.matmul_pop(acc)
        stage(0)
        lax.fori_loop(0, steps // 2, step, 0)
        pl.semaphore_wait(barrier, n - 1 + groups - 1)
        for way in range(2):
            across(way).start()
        for index in range(2):
            to_both(lambda side: early_halo(index, side).start())
        for way in range(2):
            beyond(way).start()
        lax.fori_loop(steps // 2, steps - 1, step, 0)
        accumulate(steps - 1)
        odd = lax.rem(lax.broadcasted_iota(jnp.int32, (tall, LANES), 0), 2) == 1
        for unit in range(2):
            value = pltpu.matmul_pop(accs[unit])
            picked[pl.ds(unit * tall, tall)] = jnp.where(odd, value[:, LANES:], value[:, :LANES])

    pl.run_scoped(
        lambda *accs: multiply(accs),
        pltpu.ACC(0)((tall, 2 * LANES), F32), pltpu.ACC(1)((tall, 2 * LANES), F32),
    )
    count = picked.shape[0] // 2
    turned = (picked[pl.ds(0, count, stride=2)] + picked[pl.ds(1, count, stride=2)]).T
    split, columns = SPLIT * nb, BASIS * nb
    sketched = jnp.concatenate([turned[:split] + turned[columns:], turned[split:columns]], axis=0)
    chunks = count // LANES
    flat_out = out_buf.reshape(chunks * columns, LANES)
    for r in range(chunks):
        flat_out[pl.ds(r * columns, columns)] = sketched[:, r * LANES : (r + 1) * LANES]
    parts = n // nb
    span = chunks // parts

    def piece(dest):
        return out_buf.at[pl.ds(dest // nb * span, span), :, lax.rem(dest, nb)]

    def scatter(t):
        dest = wrapped(me + t, n)
        return remote(
            piece(dest), in_buf.at[me, :, pl.ds(0, BASIS)], rs_send.at[0], rs_recv.at[0], dom=dest
        )

    for t in range(1, n):
        scatter(t).start()
    in_buf[me, :, pl.ds(0, BASIS)] = piece(me)[...]

    def clear(at):
        for index in range(groups - 1):
            wide[index, at] = jnp.zeros((depth, nb, LANES), F32)

    pl.when(jnp.logical_not(has_left))(lambda: clear(pl.ds(0, depth)))
    pl.when(jnp.logical_not(has_right))(lambda: clear(pl.ds(depth + rows, depth)))
    for index in range(2):
        wide[index, pl.ds(depth + index * half, half)] = passed_ref[index]
    for j in range(shifts):
        step_ref[j] = table_ref[ids_ref[j]] * mass1_ref[...] - kappa_ref[...]

    def images(field, slot):
        for p in range(planes - 2):
            near[pl.ds(p * ny, ny)] = neighbour_sum(field, p + 1, ny)

        def one_shift(j, carry):
            for p in range(planes - 2):
                at = pl.ds(p * ny, ny)
                flag = edge_flag(p, planes - 2, 2, low, high)
                first[at] = masked(step_ref[j, at] * plane_of(field, p + 1, ny) - near[at], flag)
            for p in range(planes - 4):
                at = pl.ds((p + 1) * ny, ny)
                flag = edge_flag(p, planes - 4, 1, low, high)
                second[pl.ds(p * ny, ny)] = masked(
                    step_ref[j, at] * first[at] - neighbour_sum(first, p + 1, ny), flag
                )
            for p in range(slab):
                at, inner, out = pl.ds((p + 2) * ny, ny), pl.ds((p + 1) * ny, ny), pl.ds(p * ny, ny)
                fields_out[slot, j, 0, out] = first[at]
                fields_out[slot, j, 1, out] = second[inner]
                fields_out[slot, j, 2, out] = (
                    step_ref[j, at] * second[inner] - neighbour_sum(second, p + 1, ny)
                )
            return carry

        lax.fori_loop(0, shifts, one_shift, 0)
        for p in range(slab):
            own_out[slot, pl.ds(p * ny, ny)] = plane_of(field, p + HALO, ny)

    images(own_ref, group)
    for way in range(2):
        across(way).wait_recv()
        to_both(lambda side: late_halo(way, side).start())

    peers = pl.ds(0, n - 1)
    drain(in_buf.at[peers, :, pl.ds(0, BASIS)], rs_recv.at[0])
    flat_in = in_buf.reshape(n * span * in_buf.shape[2], LANES)
    tile = span * in_buf.shape[2]
    total = flat_in[pl.ds(0, tile)]
    for t in range(1, n):
        total = total + flat_in[pl.ds(t * tile, tile)]
    lane = lax.broadcasted_iota(jnp.int32, (BASIS, LANES), 1)
    place = lax.broadcasted_iota(jnp.int32, (BASIS, LANES), 0)
    views = [total[r * in_buf.shape[2] :][:BASIS] for r in range(span)]
    twice = [jnp.concatenate([view, view], axis=0) for view in views]
    packed = jnp.zeros((BASIS, LANES), F32)
    for d in range(BASIS // 2 + 1):
        terms = sum(view * wrap[d : d + BASIS] for view, wrap in zip(views, twice))
        packed = jnp.where(lane == place + BASIS * d, jnp.sum(terms, axis=1, keepdims=True), packed)
    rows_buf[group, me] = jnp.sum(packed, axis=0, keepdims=True)

    def share(t):
        return remote(
            rows_buf.at[group, me], rows_buf.at[group, me], g_send.at[0], g_recv.at[0],
            dom=wrapped(me + t, n),
        )

    for t in range(1, n):
        share(t).start()
    drain(wide.at[2, pl.ds(depth, rows)], z_recv.at[2])
    to_both(lambda side: late_halo(2, side).start())
    take_halo(0)
    images(wide.at[0], slots[0])
    take_halo(1)
    images(wide.at[1], slots[1])
    drain(rows_buf.at[0, peers], g_recv.at[0])

    def spread(t):
        return remote(
            rows_buf.at[group], rows_buf.at[group], s_send.at[0], s_recv.at[0], shift=around[t]
        )

    for t in range(1, groups):
        spread(t).start()
    take_halo(2)
    images(wide.at[2], slots[2])
    others = pl.ds(0, groups - 1)
    drain(rows_buf.at[others], s_recv.at[0])

    lane_row = lax.broadcasted_iota(jnp.int32, (1, LANES), 1)
    sigma = jnp.full((1, LANES), MID, F32)
    for j in range(shifts):
        sigma = jnp.where(lane_row == j, table_ref[ids_ref[j]], sigma)
    flat_rows = rows_buf.reshape(groups * n, LANES)
    gram = []
    for g in range(groups):
        block = flat_rows[pl.ds(g * n, n)]
        gram.append(sum(block[q * nb : (q + 1) * nb] for q in range(parts)))
    solved = coefficients(jnp.concatenate(gram, axis=0), sigma)
    for i, value in enumerate(solved):
        for j in range(shifts):
            spreaded = jnp.broadcast_to(value[:, j : j + 1], value.shape)
            coeff_out[j, i] = spreaded.reshape(groups, nb, LANES)

    to_both(lambda side: drain(wide.at[:, pl.ds(0, depth)], halo_send.at[side]))
    drain(wide.at[pl.ds(0, 2), pl.ds(0, rows)], z_send.at[0])
    drain(in_buf.at[peers, :, pl.ds(0, BASIS)], rs_send.at[0])
    drain(rows_buf.at[0, peers], g_send.at[0])
    drain(rows_buf.at[others], s_send.at[0])


def combine_kernel(fields_ref, own_ref, coeff_ref, sol_hbm, res_hbm, sol_buf, res_buf, sem):
    groups, shifts = fields_ref.shape[0], fields_ref.shape[1]
    rows, nb = fields_ref.shape[3], fields_ref.shape[4]

    def copies(g, j):
        out = []
        for which, (buf, hbm) in enumerate(((sol_buf, sol_hbm), (res_buf, res_hbm))):
            for b in range(nb):
                out.append(
                    pltpu.make_async_copy(
                        buf.at[g, j, :, b], hbm.at[j, g * nb + b], sem.at[which]
                    )
                )
        return out

    def one(u, carry):
        g, j = u // shifts, lax.rem(u, shifts)
        c = [coeff_ref[j, i, g][None] for i in range(6)]
        w0 = own_ref[g]
        w1, w2, w3 = (fields_ref[g, j, i] for i in range(3))
        sol_buf.at[g, j].reshape(rows, nb, LANES)[...] = c[0] * w0 + c[1] * w1 + c[2] * w2
        res_buf.at[g, j].reshape(rows, nb, LANES)[...] = (
            c[3] * w0 - c[4] * w1 - c[5] * w2 - c[2] * w3
        )
        for copy in copies(g, j):
            copy.start()
        return carry

    lax.fori_loop(0, groups * shifts, one, 0)

    drain(sol_hbm, sem.at[0])
    drain(res_hbm, sem.at[1])


def on_device(sources, kappa, mass, shift_table, shift_ids, sketch):
    n, groups = lax.axis_size("dom"), lax.axis_size("shift")
    nb, slab, ny = sources.shape[0], sources.shape[1], sources.shape[2]
    shifts = shift_ids.shape[0]
    sk = sketch.shape[0]
    rows = slab * ny
    planes = slab + 2 * HALO
    wide_rows, inner = planes * ny, (planes - 2) * ny
    pairs = rows // 2
    weights = 2 * (BASIS + SPLIT) * nb
    vec = (nb, LANES)
    half = rows // 2
    sketch, weight, wide, passed, kappa, mass = pl.pallas_call(
        functools.partial(prepare_kernel, n, groups, ny),
        out_shape=(
            pltpu.VMEM((pairs, sk, 2, LANES), BF16),
            pltpu.VMEM((pairs, weights, LANES), BF16),
            pltpu.VMEM((wide_rows, nb, 1, LANES), F32),
            pltpu.VMEM((2, half, nb, 1, LANES), F32),
            pltpu.VMEM((inner,) + vec, F32),
            pltpu.VMEM((inner,) + vec, F32),
        ),
        in_specs=[HBM_SPEC] * 4,
        out_specs=(VMEM_SPEC,) * 6,
        scratch_shapes=[
            pltpu.VMEM((2, inner, 1, LANES), F32),
            pltpu.VMEM((inner,) + vec, F32),
            pltpu.VMEM((inner,) + vec, F32),
            pltpu.VMEM((inner,) + vec, F32),
            pltpu.VMEM((inner - 2 * ny,) + vec, F32),
            pltpu.VMEM((inner - 2 * ny,) + vec, F32),
            pltpu.VMEM((inner - 2 * ny,) + vec, F32),
            DMA((1,)), DMA((2,)),
            DMA((2,)), DMA((HALO, 2)), DMA((2,)), DMA((2,)), DMA((1,)), DMA((2,)),
        ],
        compiler_params=pltpu.CompilerParams(
            collective_id=0, has_side_effects=True, vmem_limit_bytes=16 << 20
        ),
        name="prepare",
    )(
        in_hbm(sources.reshape(nb, rows, 1, LANES)), in_hbm(kappa.reshape(rows, 1, LANES)),
        in_hbm(mass.reshape(rows, 1, LANES)), in_hbm(sketch.reshape(sk, pairs, 2, LANES)),
    )
    parts = n // nb
    span = sk // LANES // parts
    fields, own, coeff = pl.pallas_call(
        functools.partial(project_kernel, n, groups, ny),
        out_shape=(
            pltpu.VMEM((groups, shifts, 3, rows) + vec, F32),
            pltpu.VMEM((groups, rows) + vec, F32),
            pltpu.VMEM((shifts, 6, groups) + vec, F32),
        ),
        in_specs=[VMEM_SPEC] * 6 + [SMEM_SPEC] * 2,
        out_specs=(VMEM_SPEC,) * 3,
        scratch_shapes=[
            pltpu.VMEM((groups - 1, wide_rows) + vec, F32),
            pltpu.VMEM((shifts, inner) + vec, F32),
            pltpu.VMEM((2 * sk, weights // 2), F32),
            pltpu.VMEM((inner,) + vec, F32),
            pltpu.VMEM((inner,) + vec, F32),
            pltpu.VMEM((inner - 2 * ny,) + vec, F32),
            pltpu.VMEM((sk // LANES, BASIS, nb, 1, LANES), F32),
            pltpu.VMEM((n, span, 16, 1, LANES), F32),
            pltpu.VMEM((groups, n, 1, LANES), F32),
            DMA((1,)), DMA((3,)), DMA((2,)), DMA((3, 2)),
            DMA((1,)), DMA((1,)), DMA((1,)), DMA((1,)), DMA((1,)), DMA((1,)),
        ],
        compiler_params=pltpu.CompilerParams(
            collective_id=1, has_side_effects=True, vmem_limit_bytes=16 << 20
        ),
        name="project",
    )(
        in_vmem(sketch.reshape(pairs, 2 * sk, LANES)), in_vmem(weight),
        in_vmem(wide.reshape((wide_rows,) + vec)), in_vmem(passed.reshape((2, half) + vec)),
        in_vmem(kappa), in_vmem(mass), shift_table, shift_ids,
    )

    out = pltpu.HBM((shifts, groups * nb, rows, 1, LANES), F32)
    buf = pltpu.VMEM((groups, shifts, rows, nb, 1, LANES), F32)
    solution, residual = pl.pallas_call(
        combine_kernel,
        out_shape=(out, out),
        in_specs=[VMEM_SPEC] * 3,
        out_specs=(HBM_SPEC,) * 2,
        scratch_shapes=[buf, buf, DMA((2,))],
        compiler_params=pltpu.CompilerParams(vmem_limit_bytes=16 << 20),
        name="combine",
    )(in_vmem(fields), in_vmem(own), in_vmem(coeff))
    shape = (shifts, groups * nb, slab, ny, LANES)
    return solution.reshape(shape), residual.reshape(shape)


def solution(mesh):
    placed = (
        P("shift", "dom", None, None),
        P("dom", None, None),
        P("dom", None, None),
        P(),
        P("shift"),
        P(None, "dom", None, None),
    )
    return jax.shard_map(
        on_device,
        mesh=mesh,
        in_specs=placed,
        out_specs=(P("shift", None, "dom", None, None), P("shift", None, "dom", None, None)),
        check_vma=False,
    )
```

time: 47.4 us -> 40.7 us (0.86)
  Pallas kernels: 46.6 us -> 39.8 us
    pallas_call x1, Pallas kernels: 31.3 us -> 25.1 us  [on_device(): pl.pallas_call(functools.partial(project_kernel, n, groups, ny), out_shap...]
    pallas_call x1, Pallas kernels: 5.51 us -> 3.24 us  [on_device(): pl.pallas_call(combine_kernel, out_shape=(out, out), in_specs=[VMEM_SPEC]...]
    pallas_call x1, Pallas kernels: 9.82 us -> 11.4 us  [on_device(): pl.pallas_call(functools.partial(prepare_kernel, n, groups, ny), out_shap...]
where the time goes in v2:
time: 40.7 us; the launch traced here: 40.5 us
  Pallas kernels  39.8 us (98%)
  between operations  0.68 us (2%)
    pallas_call x1, Pallas kernels, on_device(): pl.pallas_call(functools.partial(project_kernel, n, groups, ny), out_shap...  25.1 us
    pallas_call x1, Pallas kernels, on_device(): pl.pallas_call(functools.partial(prepare_kernel, n, groups, ny), out_shap...  11.4 us
    pallas_call x1, Pallas kernels, on_device(): pl.pallas_call(combine_kernel, out_shape=(out, out), in_specs=[VMEM_SPEC]...  3.24 us

profile of v2, /device:TPU:1, one launch (start us, length us, event | category | flops | bytes accessed | tf_op | source)
XLA Modules:
  0.0 40.5 jit_solution(11940079417926995513)
XLA Ops:
  0.6 0.0 copy-start.1
  0.6 0.0 copy-start
  0.7 11.4 %prepare.1 = (bf16[32,1024,2,128]{3,2,1,0:T(2,128)(2,1)S(1)}, bf16[32,256,128]{2,1,0:T(8,128)(2,1)S(1)}, f32[160,8,1,128]{3,2,1,0:T(1,128)S(1)}, f32[2,32,8,1,12...) custom-call(f32[8,64,1,128]{3,2,1,0:T(1,128)} %bitcast.13, f32[64,1,128]{2,1,0:T(1,128)} %bitcast.14, ...), custom_call_target="tpu_custom_call" | custom-call | tf_op jit(solution)/shard_map/prepare/pallas_call | solution.py:639
  12.1 0.0 copy-done.1
  12.1 0.0 copy-done
  12.1 25.1 %project.1 = (f32[4,4,3,64,8,128]{5,4,3,2,1,0:T(8,128)S(1)}, f32[4,64,8,128]{3,2,1,0:T(8,128)S(1)}, f32[4,6,4,8,128]{4,3,2,1,0:T(8,128)S(1)}) custom-call(bf16[32,2048,128]{2,1,0:T(8,128)(2,1)S(1)} %bitcast.9, bf16[32,256,128]{2,1,0:T(8,128)(2,1)S(1)} %get-tuple-element.14.weights_ref, f32[160,8,128]{2,1,0:T(8,128)S(1)} %bitcast.10, ...), custom_call_target="tpu_custom_call" | custom-call | tf_op jit(solution)/shard_map/project/pallas_call | solution.py:672
  37.2 3.2 %combine.1 = (f32[4,32,64,1,128]{4,3,2,1,0:T(1,128)}, f32[4,32,64,1,128]{4,3,2,1,0:T(1,128)}) custom-call(f32[4,4,3,64,8,128]{5,4,3,2,1,0:T(8,128)S(1)} %get-tuple-element.19.fields_ref, f32[4,64,8,128]{3,2,1,0:T(8,128)S(1)} %get-tuple-element.20.own_ref, f32[4,6,4,8,128]{4,3,2,1,0:T(8,128)S(1)} %get-tuple-element.21.coeff_ref), custom_call_target="tpu_custom_call" | custom-call | tf_op jit(solution)/shard_map/combine/pallas_call | solution.py:706
Async XLA Ops:
  0.6 11.4 %copy-start.1 = (s32[4]{0:T(128)S(1)}, s32[4]{0:T(128)}, u32[]{:S(2)}) copy-start(s32[4]{0:T(128)} %ids_ref.1) | copy-start | bytes 52
  0.6 11.4 %copy-start = (f32[64]{0:T(128)S(1)}, f32[64]{0:T(128)}, u32[]{:S(2)}) copy-start(f32[64]{0:T(128)} %table_ref.1) | copy-start | bytes 772

commit v3 on v2

--- a/solution.py
+++ b/solution.py
@@ -13,6 +13,7 @@
 F32 = jnp.float32
 BF16 = jnp.bfloat16
 BASIS = 10
+LINES = 4
 SPLIT = 6
 IMAGES = ((0,), (1, 6), (2, 3, 7), (4, 5, 8, 9))
 VMEM_SPEC = pl.BlockSpec(memory_space=pltpu.VMEM)
@@ -244,7 +245,16 @@
                 level3(p)
                 done[3].add(p)
 
+    def clear_units(*accs):
+        for acc in accs:
+            pltpu.matmul_pop(acc)
+
     advance(0)
+    pl.run_scoped(
+        clear_units,
+        pltpu.ACC(0)((sketch_hbm.shape[0], 2 * LANES), F32),
+        pltpu.ACC(1)((sketch_hbm.shape[0], 2 * LANES), F32),
+    )
     pl.when(has_left)(lambda: wide_halo(0, 0).wait_recv())
     pl.when(has_right)(lambda: wide_halo(0, 1).wait_recv())
     advance(1)
@@ -339,10 +349,10 @@
 
 
 def project_kernel(
-    n, groups, ny, sketch_ref, weights_ref, own_ref, passed_ref, kappa_ref, mass1_ref, table_ref, ids_ref,
+    n, groups, lines, ny, sketch_ref, weights_ref, own_ref, passed_ref, kappa_ref, mass1_ref, table_ref, ids_ref,
     fields_out, own_out, coeff_out,
     wide, step_ref, picked, near, first, second, out_buf, in_buf, rows_buf,
-    z_send, z_recv, halo_send, halo_recv, rs_send, rs_recv, g_send, g_recv, s_send, s_recv,
+    z_send, z_recv, halo_send, halo_recv, rs_send, rs_recv, g_send, g_recv, row_sem,
 ):
     me = lax.axis_index("dom")
     group = lax.axis_index("shift")
@@ -358,8 +368,12 @@
     low, high = edge_flags(me, n)
 
     barrier = pltpu.get_barrier_semaphore()
-    for t in range(1, n):
-        signal(barrier, dom=wrapped(me + t, n))
+    row = n // lines
+    base = me // row * row
+    for t in range(1, row):
+        signal(barrier, dom=base + wrapped(me - base + t, row))
+    for t in range(1, lines):
+        signal(barrier, dom=wrapped(me + t * row, n))
     for t in range(1, groups):
         signal(barrier, shift=around[t])
 
@@ -414,7 +428,21 @@
         pl.when(has_right)(lambda: take(1))
 
     steps = sketch_ref.shape[0] // 2
-    tall = sketch_ref.shape[1] // 2
+    pieces = 2
+    tall = sketch_ref.shape[1] // (2 * pieces)
+    split, columns = SPLIT * nb, BASIS * nb
+    chunks = 2 * pieces * tall // (2 * LANES)
+    parts = n // nb
+    span = chunks // parts
+    flat_out = out_buf.reshape(chunks * columns, LANES)
+
+    def piece(dest):
+        return out_buf.at[pl.ds(dest // nb * span, span), :, lax.rem(dest, nb)]
+
+    def scatter(dest):
+        return remote(
+            piece(dest), in_buf.at[me, :, pl.ds(0, BASIS)], rs_send.at[0], rs_recv.at[0], dom=dest
+        )
 
     def stage(u):
         tile = jnp.concatenate([weights_ref[2 * u], weights_ref[2 * u + 1]], axis=1)
@@ -422,61 +450,68 @@
             pltpu.matmul_push_rhs(tile, 0, unit, transpose=True)
 
     def multiply(accs):
-        def accumulate(u):
+        def accumulate(u, part):
             for unit in range(2):
-                at = pl.ds(unit * tall, tall)
-                part = jnp.concatenate([sketch_ref[2 * u, at], sketch_ref[2 * u + 1, at]], axis=1)
-                pltpu.matmul_acc_lhs(accs[unit], part, load_staged_rhs=0)
-
-        def step(u, carry):
-            accumulate(u)
-            stage(u + 1)
-            return carry
-
-        for acc in accs:
-            pltpu.matmul_pop(acc)
+                at = pl.ds((2 * part + unit) * tall, tall)
+                tile = jnp.concatenate([sketch_ref[2 * u, at], sketch_ref[2 * u + 1, at]], axis=1)
+                pltpu.matmul_acc_lhs(accs[unit], tile, load_staged_rhs=0)
+
+        def run(part, start, stop):
+            def step(u, carry):
+                accumulate(u, part)
+                stage(u + 1)
+                return carry
+
+            lax.fori_loop(start, stop, step, 0)
+
+        def finish(part):
+            accumulate(steps - 1, part)
+            if part + 1 < pieces:
+                stage(0)
+            odd = lax.rem(lax.broadcasted_iota(jnp.int32, (tall, LANES), 0), 2) == 1
+            for unit in range(2):
+                value = pltpu.matmul_pop(accs[unit])
+                picked[pl.ds((2 * part + unit) * tall, tall)] = jnp.where(
+                    odd, value[:, LANES:], value[:, :LANES]
+                )
+            first = part * 2 * tall
+            turned = (
+                picked[pl.ds(first, tall, stride=2)] + picked[pl.ds(first + 1, tall, stride=2)]
+            ).T
+            sketched = jnp.concatenate(
+                [turned[:split] + turned[columns:], turned[split:columns]], axis=0
+            )
+            share = chunks // pieces
+            for r in range(share):
+                flat_out[pl.ds((part * share + r) * columns, columns)] = sketched[
+                    :, r * LANES : (r + 1) * LANES
+                ]
+            mine = n // pieces
+            for t in range(mine):
+                dest = part * mine + lax.rem(me + t, mine)
+                pl.when(dest != me)(lambda: scatter(dest).start())
+
         stage(0)
-        lax.fori_loop(0, steps // 2, step, 0)
-        pl.semaphore_wait(barrier, n - 1 + groups - 1)
+        run(0, 0, steps // 2)
+        pl.semaphore_wait(barrier, row - 1 + lines - 1 + groups - 1)
+        for t in range(1, lines):
+            signal(row_sem, dom=wrapped(me + t * row, n))
         for way in range(2):
             across(way).start()
+        run(0, steps // 2, steps - 1)
+        pl.semaphore_wait(row_sem, lines - 1)
+        finish(0)
         for index in range(2):
             to_both(lambda side: early_halo(index, side).start())
         for way in range(2):
             beyond(way).start()
-        lax.fori_loop(steps // 2, steps - 1, step, 0)
-        accumulate(steps - 1)
-        odd = lax.rem(lax.broadcasted_iota(jnp.int32, (tall, LANES), 0), 2) == 1
-        for unit in range(2):
-            value = pltpu.matmul_pop(accs[unit])
-            picked[pl.ds(unit * tall, tall)] = jnp.where(odd, value[:, LANES:], value[:, :LANES])
+        run(1, 0, steps - 1)
+        finish(1)
 
     pl.run_scoped(
         lambda *accs: multiply(accs),
         pltpu.ACC(0)((tall, 2 * LANES), F32), pltpu.ACC(1)((tall, 2 * LANES), F32),
     )
-    count = picked.shape[0] // 2
-    turned = (picked[pl.ds(0, count, stride=2)] + picked[pl.ds(1, count, stride=2)]).T
-    split, columns = SPLIT * nb, BASIS * nb
-    sketched = jnp.concatenate([turned[:split] + turned[columns:], turned[split:columns]], axis=0)
-    chunks = count // LANES
-    flat_out = out_buf.reshape(chunks * columns, LANES)
-    for r in range(chunks):
-        flat_out[pl.ds(r * columns, columns)] = sketched[:, r * LANES : (r + 1) * LANES]
-    parts = n // nb
-    span = chunks // parts
-
-    def piece(dest):
-        return out_buf.at[pl.ds(dest // nb * span, span), :, lax.rem(dest, nb)]
-
-    def scatter(t):
-        dest = wrapped(me + t, n)
-        return remote(
-            piece(dest), in_buf.at[me, :, pl.ds(0, BASIS)], rs_send.at[0], rs_recv.at[0], dom=dest
-        )
-
-    for t in range(1, n):
-        scatter(t).start()
     in_buf[me, :, pl.ds(0, BASIS)] = piece(me)[...]
 
     def clear(at):
@@ -538,35 +573,29 @@
     for d in range(BASIS // 2 + 1):
         terms = sum(view * wrap[d : d + BASIS] for view, wrap in zip(views, twice))
         packed = jnp.where(lane == place + BASIS * d, jnp.sum(terms, axis=1, keepdims=True), packed)
-    rows_buf[group, me] = jnp.sum(packed, axis=0, keepdims=True)
-
-    def share(t):
+    slot = group * n + me
+    rows_buf[slot] = jnp.sum(packed, axis=0, keepdims=True)
+
+    def share(t, z):
         return remote(
-            rows_buf.at[group, me], rows_buf.at[group, me], g_send.at[0], g_recv.at[0],
-            dom=wrapped(me + t, n),
-        )
-
-    for t in range(1, n):
-        share(t).start()
+            rows_buf.at[slot], rows_buf.at[slot], g_send.at[0], g_recv.at[0],
+            dom=wrapped(me + t, n), shift=around[z],
+        )
+
+    for z in (2, 1, 3, 0):
+        for t in range(n):
+            if z or t:
+                share(t, z).start()
     drain(wide.at[2, pl.ds(depth, rows)], z_recv.at[2])
     to_both(lambda side: late_halo(2, side).start())
     take_halo(0)
     images(wide.at[0], slots[0])
     take_halo(1)
     images(wide.at[1], slots[1])
-    drain(rows_buf.at[0, peers], g_recv.at[0])
-
-    def spread(t):
-        return remote(
-            rows_buf.at[group], rows_buf.at[group], s_send.at[0], s_recv.at[0], shift=around[t]
-        )
-
-    for t in range(1, groups):
-        spread(t).start()
     take_halo(2)
     images(wide.at[2], slots[2])
-    others = pl.ds(0, groups - 1)
-    drain(rows_buf.at[others], s_recv.at[0])
+    everyone = pl.ds(0, groups * n - 1)
+    drain(rows_buf.at[everyone], g_recv.at[0])
 
     lane_row = lax.broadcasted_iota(jnp.int32, (1, LANES), 1)
     sigma = jnp.full((1, LANES), MID, F32)
@@ -586,8 +615,7 @@
     to_both(lambda side: drain(wide.at[:, pl.ds(0, depth)], halo_send.at[side]))
     drain(wide.at[pl.ds(0, 2), pl.ds(0, rows)], z_send.at[0])
     drain(in_buf.at[peers, :, pl.ds(0, BASIS)], rs_send.at[0])
-    drain(rows_buf.at[0, peers], g_send.at[0])
-    drain(rows_buf.at[others], s_send.at[0])
+    drain(rows_buf.at[everyone], g_send.at[0])
 
 
 def combine_kernel(fields_ref, own_ref, coeff_ref, sol_hbm, res_hbm, sol_buf, res_buf, sem):
@@ -670,7 +698,7 @@
     parts = n // nb
     span = sk // LANES // parts
     fields, own, coeff = pl.pallas_call(
-        functools.partial(project_kernel, n, groups, ny),
+        functools.partial(project_kernel, n, groups, LINES, ny),
         out_shape=(
             pltpu.VMEM((groups, shifts, 3, rows) + vec, F32),
             pltpu.VMEM((groups, rows) + vec, F32),
@@ -687,9 +715,9 @@
             pltpu.VMEM((inner - 2 * ny,) + vec, F32),
             pltpu.VMEM((sk // LANES, BASIS, nb, 1, LANES), F32),
             pltpu.VMEM((n, span, 16, 1, LANES), F32),
-            pltpu.VMEM((groups, n, 1, LANES), F32),
+            pltpu.VMEM((groups * n, 1, LANES), F32),
             DMA((1,)), DMA((3,)), DMA((2,)), DMA((3, 2)),
-            DMA((1,)), DMA((1,)), DMA((1,)), DMA((1,)), DMA((1,)), DMA((1,)),
+            DMA((1,)), DMA((1,)), DMA((1,)), DMA((1,)), pltpu.SemaphoreType.REGULAR,
         ],
         compiler_params=pltpu.CompilerParams(
             collective_id=1, has_side_effects=True, vmem_limit_bytes=16 << 20

time: 40.7 us -> 41.8 us (1.027)
  Pallas kernels: 39.8 us -> 40.7 us
    pallas_call x1, Pallas kernels: 25.1 us -> 26 us  [on_device(): pl.pallas_call(functools.partial(project_kernel, n, groups, LINES, ny), o...]
where the time goes in v3:
time: 41.8 us; the launch traced here: 41.4 us
  Pallas kernels  40.7 us (97%)
  between operations  0.68 us (2%)
    pallas_call x1, Pallas kernels, on_device(): pl.pallas_call(functools.partial(project_kernel, n, groups, LINES, ny), o...  26 us
    pallas_call x1, Pallas kernels, on_device(): pl.pallas_call(functools.partial(prepare_kernel, n, groups, ny), out_shap...  11.4 us
    pallas_call x1, Pallas kernels, on_device(): pl.pallas_call(combine_kernel, out_shape=(out, out), in_specs=[VMEM_SPEC]...  3.24 us

profile of v3, /device:TPU:1, one launch (start us, length us, event | category | flops | bytes accessed | tf_op | source)
XLA Modules:
  0.0 41.4 jit_solution(2494008864441687987)
XLA Ops:
  0.6 0.0 copy-start.1
  0.6 0.0 copy-start
  0.7 11.4 %prepare.1 = (bf16[32,1024,2,128]{3,2,1,0:T(2,128)(2,1)S(1)}, bf16[32,256,128]{2,1,0:T(8,128)(2,1)S(1)}, f32[160,8,1,128]{3,2,1,0:T(1,128)S(1)}, f32[2,32,8,1,12...) custom-call(f32[8,64,1,128]{3,2,1,0:T(1,128)} %bitcast.13, f32[64,1,128]{2,1,0:T(1,128)} %bitcast.14, ...), custom_call_target="tpu_custom_call" | custom-call | tf_op jit(solution)/shard_map/prepare/pallas_call | solution.py:667
  12.1 0.0 copy-done.1
  12.1 0.0 copy-done
  12.1 26.0 %project.1 = (f32[4,4,3,64,8,128]{5,4,3,2,1,0:T(8,128)S(1)}, f32[4,64,8,128]{3,2,1,0:T(8,128)S(1)}, f32[4,6,4,8,128]{4,3,2,1,0:T(8,128)S(1)}) custom-call(bf16[32,2048,128]{2,1,0:T(8,128)(2,1)S(1)} %bitcast.9, bf16[32,256,128]{2,1,0:T(8,128)(2,1)S(1)} %get-tuple-element.14.weights_ref, f32[160,8,128]{2,1,0:T(8,128)S(1)} %bitcast.10, ...), custom_call_target="tpu_custom_call" | custom-call | tf_op jit(solution)/shard_map/project/pallas_call | solution.py:700
  38.1 3.2 %combine.1 = (f32[4,32,64,1,128]{4,3,2,1,0:T(1,128)}, f32[4,32,64,1,128]{4,3,2,1,0:T(1,128)}) custom-call(f32[4,4,3,64,8,128]{5,4,3,2,1,0:T(8,128)S(1)} %get-tuple-element.19.fields_ref, f32[4,64,8,128]{3,2,1,0:T(8,128)S(1)} %get-tuple-element.20.own_ref, f32[4,6,4,8,128]{4,3,2,1,0:T(8,128)S(1)} %get-tuple-element.21.coeff_ref), custom_call_target="tpu_custom_call" | custom-call | tf_op jit(solution)/shard_map/combine/pallas_call | solution.py:734
Async XLA Ops:
  0.6 11.4 %copy-start.1 = (s32[4]{0:T(128)S(1)}, s32[4]{0:T(128)}, u32[]{:S(2)}) copy-start(s32[4]{0:T(128)} %ids_ref.1) | copy-start | bytes 52
  0.6 11.4 %copy-start = (f32[64]{0:T(128)S(1)}, f32[64]{0:T(128)}, u32[]{:S(2)}) copy-start(f32[64]{0:T(128)} %table_ref.1) | copy-start | bytes 772

commit v4 on v3

--- a/solution.py
+++ b/solution.py
@@ -13,6 +13,7 @@
 F32 = jnp.float32
 BF16 = jnp.bfloat16
 BASIS = 10
+PASSED = 3
 LINES = 4
 SPLIT = 6
 IMAGES = ((0,), (1, 6), (2, 3, 7), (4, 5, 8, 9))
@@ -120,8 +121,7 @@
         return pltpu.make_async_copy(sketch_hbm.at[:, k], sketch_out.at[k], load_sem.at[0])
 
     loads = sketch_hbm.shape[1]
-    early = 6
-    for k in range(early):
+    for k in range(loads):
         load(k).start()
     drain(wide.at[pl.ds(depth, rows)], in_sem.at[0])
     drain(coef.at[:, pl.ds(thin, rows)], in_sem.at[1])
@@ -147,7 +147,7 @@
         count = passed_out.shape[1]
         there = (up, down)[way]
         return remote(
-            wide.at[pl.ds(depth + way * count, count)], passed_out.at[way],
+            wide.at[pl.ds(depth + way * (rows - count), count)], passed_out.at[way],
             z_send.at[0], z_recv.at[way], shift=there,
         )
 
@@ -163,8 +163,6 @@
     pl.when(has_left)(lambda: send_halo(1))
     for way in range(2):
         pass_on(way).start()
-    for k in range(early, loads):
-        load(k).start()
 
     field = wide.reshape(wide.shape[0], nb, LANES)
 
@@ -279,7 +277,7 @@
 
     pl.when(has_right)(lambda: sent(0))
     pl.when(has_left)(lambda: sent(1))
-    drain(wide.at[pl.ds(depth, rows)], z_send.at[0])
+    drain(wide.at[pl.ds(0, 2 * passed_out.shape[1])], z_send.at[0])
 
 
 def solve_small(h_vals, entry):
@@ -378,18 +376,31 @@
         signal(barrier, shift=around[t])
 
     slots = (down, up, around[groups // 2])
-    half = passed_ref.shape[1]
+    came = passed_ref.shape[1]
+    before = (range(came // ny), range(slab - came // ny, slab))
+    half = slab // 2
+
+    def planes_at(start, count):
+        return pl.ds(depth + start * ny, count * ny)
 
     def across(way):
-        at = pl.ds(depth + (1 - way) * half, half)
+        at = planes_at((slab - 1, 0)[way] - (1 - way) * (slab - 1 - came // ny), slab - came // ny)
         return remote(
             own_ref.at[at], wide.at[way, at], z_send.at[0], z_recv.at[way], shift=(up, down)[way]
         )
 
     def beyond(way):
+        at = pl.ds((way * half - before[way][0]) * ny, half * ny)
         return remote(
-            passed_ref.at[way], wide.at[2, pl.ds(depth + way * half, half)],
+            passed_ref.at[way, at], wide.at[2, planes_at(way * half, half)],
             z_send.at[0], z_recv.at[2], shift=(up, down)[way],
+        )
+
+    def beside(way):
+        at = pl.ds((depth + rows, 0)[way], depth)
+        return remote(
+            own_ref.at[at], wide.at[way, at], z_send.at[0], z_recv.at[3 + way],
+            shift=(up, down)[way],
         )
 
     def halo(index, side, src, first_plane, count):
@@ -403,18 +414,17 @@
         return range(slab - HALO, slab) if side == 0 else range(HALO)
 
     def early_halo(index, side):
-        held = range(index * slab // 2, (index + 1) * slab // 2)
-        mine = [p for p in planes_for(side) if p in held]
-        at = pl.ds((mine[0] - held[0]) * ny, len(mine) * ny)
-        return halo(index, side, passed_ref.at[index, at], mine[0], len(mine))
+        mine = [p for p in planes_for(side) if p in before[index]]
+        if index != side:
+            return
+        at = pl.ds((mine[0] - before[index][0]) * ny, len(mine) * ny)
+        halo(index, side, passed_ref.at[index, at], mine[0], len(mine)).start()
 
     def late_halo(index, side):
-        held = range((1 - index) * slab // 2, (2 - index) * slab // 2)
-        if index == 2:
-            held = range(slab)
-        mine = [p for p in planes_for(side) if p in held]
-        at = pl.ds(depth + mine[0] * ny, len(mine) * ny)
-        return halo(index, side, wide.at[index, at], mine[0], len(mine))
+        mine = [p for p in planes_for(side) if index == 2 or p not in before[index]]
+        if mine and index in (side, 2):
+            at = planes_at(mine[0], len(mine))
+            halo(index, side, wide.at[index, at], mine[0], len(mine)).start()
 
     def to_both(start):
         pl.when(has_right)(lambda: start(0))
@@ -424,8 +434,12 @@
         def take(side):
             drain(wide.at[index, pl.ds(0, depth)], halo_recv.at[index, side])
 
-        pl.when(has_left)(lambda: take(0))
-        pl.when(has_right)(lambda: take(1))
+        if index < 2:
+            drain(wide.at[index, pl.ds(0, depth)], z_recv.at[3 + index])
+        if index != 1:
+            pl.when(has_left)(lambda: take(0))
+        if index != 0:
+            pl.when(has_right)(lambda: take(1))
 
     steps = sketch_ref.shape[0] // 2
     pieces = 2
@@ -436,8 +450,11 @@
     span = chunks // parts
     flat_out = out_buf.reshape(chunks * columns, LANES)
 
+    def part_of(dest):
+        return lax.rem(dest, 2) * (parts // 2) + lax.rem(dest // 2, parts // 2)
+
     def piece(dest):
-        return out_buf.at[pl.ds(dest // nb * span, span), :, lax.rem(dest, nb)]
+        return out_buf.at[pl.ds(part_of(dest) * span, span), :, dest // parts]
 
     def scatter(dest):
         return remote(
@@ -488,7 +505,7 @@
                 ]
             mine = n // pieces
             for t in range(mine):
-                dest = part * mine + lax.rem(me + t, mine)
+                dest = pieces * lax.rem(me // pieces + t, mine) + part
                 pl.when(dest != me)(lambda: scatter(dest).start())
 
         stage(0)
@@ -498,13 +515,15 @@
             signal(row_sem, dom=wrapped(me + t * row, n))
         for way in range(2):
             across(way).start()
+        for way in range(2):
+            beyond(way).start()
+        for way in range(2):
+            beside(way).start()
         run(0, steps // 2, steps - 1)
         pl.semaphore_wait(row_sem, lines - 1)
+        for index in range(2):
+            to_both(lambda side: early_halo(index, side))
         finish(0)
-        for index in range(2):
-            to_both(lambda side: early_halo(index, side).start())
-        for way in range(2):
-            beyond(way).start()
         run(1, 0, steps - 1)
         finish(1)
 
@@ -514,108 +533,155 @@
     )
     in_buf[me, :, pl.ds(0, BASIS)] = piece(me)[...]
 
-    def clear(at):
-        for index in range(groups - 1):
+    def clear(at, indices):
+        for index in indices:
             wide[index, at] = jnp.zeros((depth, nb, LANES), F32)
 
-    pl.when(jnp.logical_not(has_left))(lambda: clear(pl.ds(0, depth)))
-    pl.when(jnp.logical_not(has_right))(lambda: clear(pl.ds(depth + rows, depth)))
+    pl.when(jnp.logical_not(has_left))(lambda: clear(pl.ds(0, depth), (0, 2)))
+    pl.when(jnp.logical_not(has_right))(lambda: clear(pl.ds(depth + rows, depth), (1, 2)))
     for index in range(2):
-        wide[index, pl.ds(depth + index * half, half)] = passed_ref[index]
+        wide[index, planes_at(before[index][0], came // ny)] = passed_ref[index]
     for j in range(shifts):
         step_ref[j] = table_ref[ids_ref[j]] * mass1_ref[...] - kappa_ref[...]
 
-    def images(field, slot):
-        for p in range(planes - 2):
-            near[pl.ds(p * ny, ny)] = neighbour_sum(field, p + 1, ny)
-
-        def one_shift(j, carry):
-            for p in range(planes - 2):
-                at = pl.ds(p * ny, ny)
-                flag = edge_flag(p, planes - 2, 2, low, high)
-                first[at] = masked(step_ref[j, at] * plane_of(field, p + 1, ny) - near[at], flag)
-            for p in range(planes - 4):
-                at = pl.ds((p + 1) * ny, ny)
-                flag = edge_flag(p, planes - 4, 1, low, high)
-                second[pl.ds(p * ny, ny)] = masked(
-                    step_ref[j, at] * first[at] - neighbour_sum(first, p + 1, ny), flag
-                )
-            for p in range(slab):
-                at, inner, out = pl.ds((p + 2) * ny, ny), pl.ds((p + 1) * ny, ny), pl.ds(p * ny, ny)
-                fields_out[slot, j, 0, out] = first[at]
-                fields_out[slot, j, 1, out] = second[inner]
-                fields_out[slot, j, 2, out] = (
-                    step_ref[j, at] * second[inner] - neighbour_sum(second, p + 1, ny)
-                )
+    def split_sums(field, at, acc):
+        parts_of = [field[pl.ds(p * ny, ny)].reshape(ny * nb, LANES) for p in at]
+        high_parts = [part.astype(BF16) for part in parts_of]
+        low_parts = [
+            (part - high_part.astype(F32)).astype(BF16)
+            for part, high_part in zip(parts_of, high_parts)
+        ]
+        pltpu.matmul_acc_lhs(acc, jnp.concatenate(high_parts, axis=1))
+        pltpu.matmul_acc_lhs(acc, jnp.concatenate(low_parts, axis=1))
+
+    def plane_sum(field, p):
+        inner = plane_of(field, p, ny)
+        total = plane_of(field, p - 1, ny) + plane_of(field, p + 1, ny)
+        none = jnp.zeros((1,) + inner.shape[1:], F32)
+        total = total + jnp.concatenate([none, inner[:-1]], axis=0)
+        return total + jnp.concatenate([inner[1:], none], axis=0)
+
+    def neighbour_sums(field, start, stop, accs):
+        pairs = [(p, p + 1) for p in range(start, stop, 2)]
+        for pair, acc in zip(pairs, accs):
+            split_sums(field, pair, acc)
+        across_planes = [plane_sum(field, p) for p in range(start, stop)]
+        for pair, acc in zip(pairs, accs):
+            value = pltpu.matmul_pop(acc)
+            for i, p in enumerate(pair):
+                along = value[:, i * LANES : (i + 1) * LANES].reshape(ny, nb, LANES)
+                yield p, across_planes[p - start] + along
+
+    def images(field, slot, accs):
+        for p, total in neighbour_sums(field, 1, planes - 1, accs[0]):
+            near[pl.ds((p - 1) * ny, ny)] = total
+
+        def shift_pair(u, carry):
+            for i in range(2):
+                j = 2 * u + i
+                for p in range(planes - 2):
+                    at = pl.ds(p * ny, ny)
+                    flag = edge_flag(p, planes - 2, 2, low, high)
+                    first[i, at] = masked(
+                        step_ref[j, at] * plane_of(field, p + 1, ny) - near[at], flag
+                    )
+            for i in range(2):
+                j = 2 * u + i
+                for p, total in neighbour_sums(first.at[i], 1, planes - 3, accs[i]):
+                    at = pl.ds(p * ny, ny)
+                    flag = edge_flag(p - 1, planes - 4, 1, low, high)
+                    second[i, pl.ds((p - 1) * ny, ny)] = masked(
+                        step_ref[j, at] * first[i, at] - total, flag
+                    )
+            for i in range(2):
+                j = 2 * u + i
+                for p, total in neighbour_sums(second.at[i], 1, planes - 5, accs[i]):
+                    at, inner, out = (pl.ds((p + k) * ny, ny) for k in (1, 0, -1))
+                    fields_out[slot, j, 0, out] = first[i, at]
+                    fields_out[slot, j, 1, out] = second[i, inner]
+                    fields_out[slot, j, 2, out] = step_ref[j, at] * second[i, inner] - total
             return carry
 
-        lax.fori_loop(0, shifts, one_shift, 0)
+        lax.fori_loop(0, shifts // 2, shift_pair, 0)
         for p in range(slab):
             own_out[slot, pl.ds(p * ny, ny)] = plane_of(field, p + HALO, ny)
 
-    images(own_ref, group)
-    for way in range(2):
-        across(way).wait_recv()
-        to_both(lambda side: late_halo(way, side).start())
-
-    peers = pl.ds(0, n - 1)
-    drain(in_buf.at[peers, :, pl.ds(0, BASIS)], rs_recv.at[0])
-    flat_in = in_buf.reshape(n * span * in_buf.shape[2], LANES)
-    tile = span * in_buf.shape[2]
-    total = flat_in[pl.ds(0, tile)]
-    for t in range(1, n):
-        total = total + flat_in[pl.ds(t * tile, tile)]
-    lane = lax.broadcasted_iota(jnp.int32, (BASIS, LANES), 1)
-    place = lax.broadcasted_iota(jnp.int32, (BASIS, LANES), 0)
-    views = [total[r * in_buf.shape[2] :][:BASIS] for r in range(span)]
-    twice = [jnp.concatenate([view, view], axis=0) for view in views]
-    packed = jnp.zeros((BASIS, LANES), F32)
-    for d in range(BASIS // 2 + 1):
-        terms = sum(view * wrap[d : d + BASIS] for view, wrap in zip(views, twice))
-        packed = jnp.where(lane == place + BASIS * d, jnp.sum(terms, axis=1, keepdims=True), packed)
-    slot = group * n + me
-    rows_buf[slot] = jnp.sum(packed, axis=0, keepdims=True)
-
-    def share(t, z):
-        return remote(
-            rows_buf.at[slot], rows_buf.at[slot], g_send.at[0], g_recv.at[0],
-            dom=wrapped(me + t, n), shift=around[z],
-        )
-
-    for z in (2, 1, 3, 0):
-        for t in range(n):
-            if z or t:
-                share(t, z).start()
-    drain(wide.at[2, pl.ds(depth, rows)], z_recv.at[2])
-    to_both(lambda side: late_halo(2, side).start())
-    take_halo(0)
-    images(wide.at[0], slots[0])
-    take_halo(1)
-    images(wide.at[1], slots[1])
-    take_halo(2)
-    images(wide.at[2], slots[2])
-    everyone = pl.ds(0, groups * n - 1)
-    drain(rows_buf.at[everyone], g_recv.at[0])
-
-    lane_row = lax.broadcasted_iota(jnp.int32, (1, LANES), 1)
-    sigma = jnp.full((1, LANES), MID, F32)
-    for j in range(shifts):
-        sigma = jnp.where(lane_row == j, table_ref[ids_ref[j]], sigma)
-    flat_rows = rows_buf.reshape(groups * n, LANES)
-    gram = []
-    for g in range(groups):
-        block = flat_rows[pl.ds(g * n, n)]
-        gram.append(sum(block[q * nb : (q + 1) * nb] for q in range(parts)))
-    solved = coefficients(jnp.concatenate(gram, axis=0), sigma)
-    for i, value in enumerate(solved):
+    def after(*accs):
+        accs = (accs[:4], accs[4:])
+        here = lax.broadcasted_iota(jnp.int32, (2 * LANES, 2 * LANES), 0)
+        there = lax.broadcasted_iota(jnp.int32, (2 * LANES, 2 * LANES), 1)
+        beside = (jnp.abs(here - there) == 1) & (here // LANES == there // LANES)
+        neighbours = jnp.where(beside, 1.0, 0.0).astype(BF16)
+        for unit in range(2):
+            pltpu.matmul_push_rhs(neighbours, 0, unit)
+            pltpu.matmul_acc_lhs(
+                accs[0][unit], jnp.zeros((ny * nb, 2 * LANES), BF16), load_staged_rhs=0
+            )
+        for way in range(2):
+            across(way).wait_recv()
+            to_both(lambda side: late_halo(way, side))
+        images(own_ref, group, accs)
+        drain(wide.at[2, pl.ds(depth, rows)], z_recv.at[2])
+        to_both(lambda side: late_halo(2, side))
+        peers = pl.ds(0, n - 1)
+        drain(in_buf.at[peers, :, pl.ds(0, BASIS)], rs_recv.at[0])
+        flat_in = in_buf.reshape(n * span * in_buf.shape[2], LANES)
+        tile = span * in_buf.shape[2]
+        total = flat_in[pl.ds(0, tile)]
+        for t in range(1, n):
+            total = total + flat_in[pl.ds(t * tile, tile)]
+        lane = lax.broadcasted_iota(jnp.int32, (BASIS, LANES), 1)
+        place = lax.broadcasted_iota(jnp.int32, (BASIS, LANES), 0)
+        views = [total[r * in_buf.shape[2] :][:BASIS] for r in range(span)]
+        twice = [jnp.concatenate([view, view], axis=0) for view in views]
+        packed = jnp.zeros((BASIS, LANES), F32)
+        for d in range(BASIS // 2 + 1):
+            terms = sum(view * wrap[d : d + BASIS] for view, wrap in zip(views, twice))
+            packed = jnp.where(lane == place + BASIS * d, jnp.sum(terms, axis=1, keepdims=True), packed)
+        slot = group * n + part_of(me) * nb + me // parts
+        rows_buf[slot] = jnp.sum(packed, axis=0, keepdims=True)
+
+        def share(t, z):
+            return remote(
+                rows_buf.at[slot], rows_buf.at[slot], g_send.at[0], g_recv.at[0],
+                dom=wrapped(me + t, n), shift=around[z],
+            )
+
+        for z in (2, 1, 3, 0):
+            for t in range(n):
+                if z or t:
+                    share(t, z).start()
+        take_halo(0)
+        images(wide.at[0], slots[0], accs)
+        take_halo(1)
+        images(wide.at[1], slots[1], accs)
+        take_halo(2)
+        images(wide.at[2], slots[2], accs)
+        everyone = pl.ds(0, groups * n - 1)
+        drain(rows_buf.at[everyone], g_recv.at[0])
+
+        lane_row = lax.broadcasted_iota(jnp.int32, (1, LANES), 1)
+        sigma = jnp.full((1, LANES), MID, F32)
         for j in range(shifts):
-            spreaded = jnp.broadcast_to(value[:, j : j + 1], value.shape)
-            coeff_out[j, i] = spreaded.reshape(groups, nb, LANES)
-
-    to_both(lambda side: drain(wide.at[:, pl.ds(0, depth)], halo_send.at[side]))
-    drain(wide.at[pl.ds(0, 2), pl.ds(0, rows)], z_send.at[0])
-    drain(in_buf.at[peers, :, pl.ds(0, BASIS)], rs_send.at[0])
-    drain(rows_buf.at[everyone], g_send.at[0])
+            sigma = jnp.where(lane_row == j, table_ref[ids_ref[j]], sigma)
+        flat_rows = rows_buf.reshape(groups * n, LANES)
+        gram = []
+        for g in range(groups):
+            block = flat_rows[pl.ds(g * n, n)]
+            gram.append(sum(block[q * nb : (q + 1) * nb] for q in range(parts)))
+        solved = coefficients(jnp.concatenate(gram, axis=0), sigma)
+        for i, value in enumerate(solved):
+            for j in range(shifts):
+                spreaded = jnp.broadcast_to(value[:, j : j + 1], value.shape)
+                coeff_out[j, i] = spreaded.reshape(groups, nb, LANES)
+
+        to_both(lambda side: drain(wide.at[pl.ds(0, 2), pl.ds(0, depth)], halo_send.at[side]))
+        drain(wide.at[pl.ds(0, 2), pl.ds(0, rows - came + half * ny + depth)], z_send.at[0])
+        drain(in_buf.at[peers, :, pl.ds(0, BASIS)], rs_send.at[0])
+        drain(rows_buf.at[everyone], g_send.at[0])
+
+    unit_sums = [pltpu.ACC(i % 2)((ny * nb, 2 * LANES), F32) for i in range(8)]
+    pl.run_scoped(after, *unit_sums)
 
 
 def combine_kernel(fields_ref, own_ref, coeff_ref, sol_hbm, res_hbm, sol_buf, res_buf, sem):
@@ -663,14 +729,14 @@
     pairs = rows // 2
     weights = 2 * (BASIS + SPLIT) * nb
     vec = (nb, LANES)
-    half = rows // 2
+    held = PASSED * ny
     sketch, weight, wide, passed, kappa, mass = pl.pallas_call(
         functools.partial(prepare_kernel, n, groups, ny),
         out_shape=(
             pltpu.VMEM((pairs, sk, 2, LANES), BF16),
             pltpu.VMEM((pairs, weights, LANES), BF16),
             pltpu.VMEM((wide_rows, nb, 1, LANES), F32),
-            pltpu.VMEM((2, half, nb, 1, LANES), F32),
+            pltpu.VMEM((2, held, nb, 1, LANES), F32),
             pltpu.VMEM((inner,) + vec, F32),
             pltpu.VMEM((inner,) + vec, F32),
         ),
@@ -711,12 +777,12 @@
             pltpu.VMEM((shifts, inner) + vec, F32),
             pltpu.VMEM((2 * sk, weights // 2), F32),
             pltpu.VMEM((inner,) + vec, F32),
-            pltpu.VMEM((inner,) + vec, F32),
-            pltpu.VMEM((inner - 2 * ny,) + vec, F32),
+            pltpu.VMEM((2, inner) + vec, F32),
+            pltpu.VMEM((2, inner - 2 * ny) + vec, F32),
             pltpu.VMEM((sk // LANES, BASIS, nb, 1, LANES), F32),
             pltpu.VMEM((n, span, 16, 1, LANES), F32),
             pltpu.VMEM((groups * n, 1, LANES), F32),
-            DMA((1,)), DMA((3,)), DMA((2,)), DMA((3, 2)),
+            DMA((1,)), DMA((5,)), DMA((2,)), DMA((3, 2)),
             DMA((1,)), DMA((1,)), DMA((1,)), DMA((1,)), pltpu.SemaphoreType.REGULAR,
         ],
         compiler_params=pltpu.CompilerParams(
@@ -725,7 +791,7 @@
         name="project",
     )(
         in_vmem(sketch.reshape(pairs, 2 * sk, LANES)), in_vmem(weight),
-        in_vmem(wide.reshape((wide_rows,) + vec)), in_vmem(passed.reshape((2, half) + vec)),
+        in_vmem(wide.reshape((wide_rows,) + vec)), in_vmem(passed.reshape((2, held) + vec)),
         in_vmem(kappa), in_vmem(mass), shift_table, shift_ids,
     )
 

time: 41.8 us -> 37.9 us (0.907)
  Pallas kernels: 40.7 us -> 37.1 us
    pallas_call x1, Pallas kernels: 26 us -> 22 us  [on_device(): pl.pallas_call(functools.partial(project_kernel, n, groups, LINES, ny), o...]
    pallas_call x1, Pallas kernels: 11.4 us -> 11.9 us  [on_device(): pl.pallas_call(functools.partial(prepare_kernel, n, groups, ny), out_shap...]
where the time goes in v4:
time: 37.9 us; the launch traced here: 37.8 us
  Pallas kernels  37.1 us (98%)
  between operations  0.68 us (2%)
    pallas_call x1, Pallas kernels, on_device(): pl.pallas_call(functools.partial(project_kernel, n, groups, LINES, ny), o...  22 us
    pallas_call x1, Pallas kernels, on_device(): pl.pallas_call(functools.partial(prepare_kernel, n, groups, ny), out_shap...  11.9 us
    pallas_call x1, Pallas kernels, on_device(): pl.pallas_call(combine_kernel, out_shape=(out, out), in_specs=[VMEM_SPEC]...  3.24 us

profile of v4, /device:TPU:1, one launch (start us, length us, event | category | flops | bytes accessed | tf_op | source)
XLA Modules:
  0.0 37.8 jit_solution(2801185843415542781)
XLA Ops:
  0.6 0.0 copy-start.1
  0.6 0.0 copy-start
  0.7 11.9 %prepare.1 = (bf16[32,1024,2,128]{3,2,1,0:T(2,128)(2,1)S(1)}, bf16[32,256,128]{2,1,0:T(8,128)(2,1)S(1)}, f32[160,8,1,128]{3,2,1,0:T(1,128)S(1)}, f32[2,48,8,1,12...) custom-call(f32[8,64,1,128]{3,2,1,0:T(1,128)} %bitcast.13, f32[64,1,128]{2,1,0:T(1,128)} %bitcast.14, ...), custom_call_target="tpu_custom_call" | custom-call | tf_op jit(solution)/shard_map/prepare/pallas_call | solution.py:733
  12.6 0.0 copy-done.1
  12.6 0.0 copy-done
  12.6 22.0 %project.1 = (f32[4,4,3,64,8,128]{5,4,3,2,1,0:T(8,128)S(1)}, f32[4,64,8,128]{3,2,1,0:T(8,128)S(1)}, f32[4,6,4,8,128]{4,3,2,1,0:T(8,128)S(1)}) custom-call(bf16[32,2048,128]{2,1,0:T(8,128)(2,1)S(1)} %bitcast.9, bf16[32,256,128]{2,1,0:T(8,128)(2,1)S(1)} %get-tuple-element.14.weights_ref, f32[160,8,128]{2,1,0:T(8,128)S(1)} %bitcast.10, ...), custom_call_target="tpu_custom_call" | custom-call | tf_op jit(solution)/shard_map/project/pallas_call | solution.py:766
  34.6 3.2 %combine.1 = (f32[4,32,64,1,128]{4,3,2,1,0:T(1,128)}, f32[4,32,64,1,128]{4,3,2,1,0:T(1,128)}) custom-call(f32[4,4,3,64,8,128]{5,4,3,2,1,0:T(8,128)S(1)} %get-tuple-element.19.fields_ref, f32[4,64,8,128]{3,2,1,0:T(8,128)S(1)} %get-tuple-element.20.own_ref, f32[4,6,4,8,128]{4,3,2,1,0:T(8,128)S(1)} %get-tuple-element.21.coeff_ref), custom_call_target="tpu_custom_call" | custom-call | tf_op jit(solution)/shard_map/combine/pallas_call | solution.py:800
Async XLA Ops:
  0.6 11.9 %copy-start.1 = (s32[4]{0:T(128)S(1)}, s32[4]{0:T(128)}, u32[]{:S(2)}) copy-start(s32[4]{0:T(128)} %ids_ref.1) | copy-start | bytes 52
  0.6 11.9 %copy-start = (f32[64]{0:T(128)S(1)}, f32[64]{0:T(128)}, u32[]{:S(2)}) copy-start(f32[64]{0:T(128)} %table_ref.1) | copy-start | bytes 772

commit v5 on v4

--- a/solution.py
+++ b/solution.py
@@ -403,6 +403,12 @@
             shift=(up, down)[way],
         )
 
+    def relay(way):
+        at = pl.ds((depth + rows, 0)[way], depth)
+        return remote(
+            wide.at[way, at], wide.at[2, at], z_send.at[0], z_recv.at[5 + way], shift=(up, down)[way]
+        )
+
     def halo(index, side, src, first_plane, count):
         target = ((first_plane - (slab - HALO)) * ny, depth + rows + first_plane * ny)[side]
         return remote(
@@ -421,8 +427,8 @@
         halo(index, side, passed_ref.at[index, at], mine[0], len(mine)).start()
 
     def late_halo(index, side):
-        mine = [p for p in planes_for(side) if index == 2 or p not in before[index]]
-        if mine and index in (side, 2):
+        mine = [p for p in planes_for(side) if p not in before[index]]
+        if mine and index == side:
             at = planes_at(mine[0], len(mine))
             halo(index, side, wide.at[index, at], mine[0], len(mine)).start()
 
@@ -434,12 +440,13 @@
         def take(side):
             drain(wide.at[index, pl.ds(0, depth)], halo_recv.at[index, side])
 
-        if index < 2:
-            drain(wide.at[index, pl.ds(0, depth)], z_recv.at[3 + index])
-        if index != 1:
+        if index == 0:
             pl.when(has_left)(lambda: take(0))
-        if index != 0:
+        if index == 1:
             pl.when(has_right)(lambda: take(1))
+        if index == 2:
+            for way in range(2):
+                drain(wide.at[2, pl.ds(0, depth)], z_recv.at[5 + way])
 
     steps = sketch_ref.shape[0] // 2
     pieces = 2
@@ -481,7 +488,7 @@
 
             lax.fori_loop(start, stop, step, 0)
 
-        def finish(part):
+        def collect(part):
             accumulate(steps - 1, part)
             if part + 1 < pieces:
                 stage(0)
@@ -503,29 +510,33 @@
                 flat_out[pl.ds((part * share + r) * columns, columns)] = sketched[
                     :, r * LANES : (r + 1) * LANES
                 ]
+
+        def send(part):
             mine = n // pieces
             for t in range(mine):
                 dest = pieces * lax.rem(me // pieces + t, mine) + part
                 pl.when(dest != me)(lambda: scatter(dest).start())
 
         stage(0)
-        run(0, 0, steps // 2)
+        run(0, 0, steps - 1)
         pl.semaphore_wait(barrier, row - 1 + lines - 1 + groups - 1)
         for t in range(1, lines):
             signal(row_sem, dom=wrapped(me + t * row, n))
         for way in range(2):
             across(way).start()
         for way in range(2):
+            beside(way).start()
+        for way in range(2):
             beyond(way).start()
-        for way in range(2):
-            beside(way).start()
-        run(0, steps // 2, steps - 1)
+        collect(0)
+        run(1, 0, steps // 2)
         pl.semaphore_wait(row_sem, lines - 1)
+        send(0)
         for index in range(2):
             to_both(lambda side: early_halo(index, side))
-        finish(0)
-        run(1, 0, steps - 1)
-        finish(1)
+        run(1, steps // 2, steps - 1)
+        collect(1)
+        send(1)
 
     pl.run_scoped(
         lambda *accs: multiply(accs),
@@ -537,8 +548,8 @@
         for index in indices:
             wide[index, at] = jnp.zeros((depth, nb, LANES), F32)
 
-    pl.when(jnp.logical_not(has_left))(lambda: clear(pl.ds(0, depth), (0, 2)))
-    pl.when(jnp.logical_not(has_right))(lambda: clear(pl.ds(depth + rows, depth), (1, 2)))
+    pl.when(jnp.logical_not(has_left))(lambda: clear(pl.ds(0, depth), (0,)))
+    pl.when(jnp.logical_not(has_right))(lambda: clear(pl.ds(depth + rows, depth), (1,)))
     for index in range(2):
         wide[index, planes_at(before[index][0], came // ny)] = passed_ref[index]
     for j in range(shifts):
@@ -621,8 +632,9 @@
             across(way).wait_recv()
             to_both(lambda side: late_halo(way, side))
         images(own_ref, group, accs)
-        drain(wide.at[2, pl.ds(depth, rows)], z_recv.at[2])
-        to_both(lambda side: late_halo(2, side))
+        for way in range(2):
+            drain(wide.at[way, pl.ds(0, depth)], z_recv.at[3 + way])
+            relay(way).start()
         peers = pl.ds(0, n - 1)
         drain(in_buf.at[peers, :, pl.ds(0, BASIS)], rs_recv.at[0])
         flat_in = in_buf.reshape(n * span * in_buf.shape[2], LANES)
@@ -655,6 +667,7 @@
         images(wide.at[0], slots[0], accs)
         take_halo(1)
         images(wide.at[1], slots[1], accs)
+        drain(wide.at[2, pl.ds(depth, rows)], z_recv.at[2])
         take_halo(2)
         images(wide.at[2], slots[2], accs)
         everyone = pl.ds(0, groups * n - 1)
@@ -675,8 +688,8 @@
                 spreaded = jnp.broadcast_to(value[:, j : j + 1], value.shape)
                 coeff_out[j, i] = spreaded.reshape(groups, nb, LANES)
 
-        to_both(lambda side: drain(wide.at[pl.ds(0, 2), pl.ds(0, depth)], halo_send.at[side]))
-        drain(wide.at[pl.ds(0, 2), pl.ds(0, rows - came + half * ny + depth)], z_send.at[0])
+        to_both(lambda side: drain(wide.at[0, pl.ds(0, depth)], halo_send.at[side]))
+        drain(wide.at[pl.ds(0, 2), pl.ds(0, rows - came + half * ny + 2 * depth)], z_send.at[0])
         drain(in_buf.at[peers, :, pl.ds(0, BASIS)], rs_send.at[0])
         drain(rows_buf.at[everyone], g_send.at[0])
 
@@ -782,7 +795,7 @@
             pltpu.VMEM((sk // LANES, BASIS, nb, 1, LANES), F32),
             pltpu.VMEM((n, span, 16, 1, LANES), F32),
             pltpu.VMEM((groups * n, 1, LANES), F32),
-            DMA((1,)), DMA((5,)), DMA((2,)), DMA((3, 2)),
+            DMA((1,)), DMA((7,)), DMA((2,)), DMA((2, 2)),
             DMA((1,)), DMA((1,)), DMA((1,)), DMA((1,)), pltpu.SemaphoreType.REGULAR,
         ],
         compiler_params=pltpu.CompilerParams(

time: 37.9 us -> 37.6 us (level)
  no operation moved by 1% of the time
where the time goes in v5:
time: 37.6 us; the launch traced here: 37.4 us
  Pallas kernels  36.8 us (98%)
  between operations  0.68 us (2%)
    pallas_call x1, Pallas kernels, on_device(): pl.pallas_call(functools.partial(project_kernel, n, groups, LINES, ny), o...  21.6 us
    pallas_call x1, Pallas kernels, on_device(): pl.pallas_call(functools.partial(prepare_kernel, n, groups, ny), out_shap...  11.9 us
    pallas_call x1, Pallas kernels, on_device(): pl.pallas_call(combine_kernel, out_shape=(out, out), in_specs=[VMEM_SPEC]...  3.24 us

profile of v5, /device:TPU:1, one launch (start us, length us, event | category | flops | bytes accessed | tf_op | source)
XLA Modules:
  0.0 37.4 jit_solution(1083881467351936315)
XLA Ops:
  0.6 0.0 copy-start.1
  0.6 0.0 copy-start
  0.7 11.9 %prepare.1 = (bf16[32,1024,2,128]{3,2,1,0:T(2,128)(2,1)S(1)}, bf16[32,256,128]{2,1,0:T(8,128)(2,1)S(1)}, f32[160,8,1,128]{3,2,1,0:T(1,128)S(1)}, f32[2,48,8,1,12...) custom-call(f32[8,64,1,128]{3,2,1,0:T(1,128)} %bitcast.13, f32[64,1,128]{2,1,0:T(1,128)} %bitcast.14, ...), custom_call_target="tpu_custom_call" | custom-call | tf_op jit(solution)/shard_map/prepare/pallas_call | solution.py:746
  12.6 0.0 copy-done.1
  12.6 0.0 copy-done
  12.6 21.6 %project.1 = (f32[4,4,3,64,8,128]{5,4,3,2,1,0:T(8,128)S(1)}, f32[4,64,8,128]{3,2,1,0:T(8,128)S(1)}, f32[4,6,4,8,128]{4,3,2,1,0:T(8,128)S(1)}) custom-call(bf16[32,2048,128]{2,1,0:T(8,128)(2,1)S(1)} %bitcast.9, bf16[32,256,128]{2,1,0:T(8,128)(2,1)S(1)} %get-tuple-element.14.weights_ref, f32[160,8,128]{2,1,0:T(8,128)S(1)} %bitcast.10, ...), custom_call_target="tpu_custom_call" | custom-call | tf_op jit(solution)/shard_map/project/pallas_call | solution.py:779
  34.2 3.2 %combine.1 = (f32[4,32,64,1,128]{4,3,2,1,0:T(1,128)}, f32[4,32,64,1,128]{4,3,2,1,0:T(1,128)}) custom-call(f32[4,4,3,64,8,128]{5,4,3,2,1,0:T(8,128)S(1)} %get-tuple-element.19.fields_ref, f32[4,64,8,128]{3,2,1,0:T(8,128)S(1)} %get-tuple-element.20.own_ref, f32[4,6,4,8,128]{4,3,2,1,0:T(8,128)S(1)} %get-tuple-element.21.coeff_ref), custom_call_target="tpu_custom_call" | custom-call | tf_op jit(solution)/shard_map/combine/pallas_call | solution.py:813
Async XLA Ops:
  0.6 11.9 %copy-start.1 = (s32[4]{0:T(128)S(1)}, s32[4]{0:T(128)}, u32[]{:S(2)}) copy-start(s32[4]{0:T(128)} %ids_ref.1) | copy-start | bytes 52
  0.6 11.9 %copy-start = (f32[64]{0:T(128)S(1)}, f32[64]{0:T(128)}, u32[]{:S(2)}) copy-start(f32[64]{0:T(128)} %table_ref.1) | copy-start | bytes 772

commit v6 on v5

--- a/solution.py
+++ b/solution.py
@@ -583,9 +583,10 @@
                 along = value[:, i * LANES : (i + 1) * LANES].reshape(ny, nb, LANES)
                 yield p, across_planes[p - start] + along
 
-    def images(field, slot, accs):
-        for p, total in neighbour_sums(field, 1, planes - 1, accs[0]):
-            near[pl.ds((p - 1) * ny, ny)] = total
+    def images(field, slot, accs, start=0, stop=shifts // 2):
+        if start == 0:
+            for p, total in neighbour_sums(field, 1, planes - 1, accs[0]):
+                near[pl.ds((p - 1) * ny, ny)] = total
 
         def shift_pair(u, carry):
             for i in range(2):
@@ -613,7 +614,9 @@
                     fields_out[slot, j, 2, out] = step_ref[j, at] * second[i, inner] - total
             return carry
 
-        lax.fori_loop(0, shifts // 2, shift_pair, 0)
+        lax.fori_loop(start, stop, shift_pair, 0)
+        if stop < shifts // 2:
+            return
         for p in range(slab):
             own_out[slot, pl.ds(p * ny, ny)] = plane_of(field, p + HALO, ny)
 
@@ -635,6 +638,8 @@
         for way in range(2):
             drain(wide.at[way, pl.ds(0, depth)], z_recv.at[3 + way])
             relay(way).start()
+        take_halo(0)
+        images(wide.at[0], slots[0], accs, stop=shifts // 4)
         peers = pl.ds(0, n - 1)
         drain(in_buf.at[peers, :, pl.ds(0, BASIS)], rs_recv.at[0])
         flat_in = in_buf.reshape(n * span * in_buf.shape[2], LANES)
@@ -663,8 +668,7 @@
             for t in range(n):
                 if z or t:
                     share(t, z).start()
-        take_halo(0)
-        images(wide.at[0], slots[0], accs)
+        images(wide.at[0], slots[0], accs, start=shifts // 4)
         take_halo(1)
         images(wide.at[1], slots[1], accs)
         drain(wide.at[2, pl.ds(depth, rows)], z_recv.at[2])

time: 37.6 us -> 38.1 us (1.013)
  Pallas kernels: 36.8 us -> 37.3 us
    pallas_call x1, Pallas kernels: 21.6 us -> 22.1 us  [on_device(): pl.pallas_call(functools.partial(project_kernel, n, groups, LINES, ny), o...]
where the time goes in v6:
time: 38.1 us; the launch traced here: 38 us
  Pallas kernels  37.3 us (98%)
  between operations  0.68 us (2%)
    pallas_call x1, Pallas kernels, on_device(): pl.pallas_call(functools.partial(project_kernel, n, groups, LINES, ny), o...  22.1 us
    pallas_call x1, Pallas kernels, on_device(): pl.pallas_call(functools.partial(prepare_kernel, n, groups, ny), out_shap...  11.9 us
    pallas_call x1, Pallas kernels, on_device(): pl.pallas_call(combine_kernel, out_shape=(out, out), in_specs=[VMEM_SPEC]...  3.24 us

profile of v6, /device:TPU:1, one launch (start us, length us, event | category | flops | bytes accessed | tf_op | source)
XLA Modules:
  0.0 38.0 jit_solution(8292747974265930125)
XLA Ops:
  0.6 0.0 copy-start.1
  0.6 0.0 copy-start
  0.7 11.9 %prepare.1 = (bf16[32,1024,2,128]{3,2,1,0:T(2,128)(2,1)S(1)}, bf16[32,256,128]{2,1,0:T(8,128)(2,1)S(1)}, f32[160,8,1,128]{3,2,1,0:T(1,128)S(1)}, f32[2,48,8,1,12...) custom-call(f32[8,64,1,128]{3,2,1,0:T(1,128)} %bitcast.13, f32[64,1,128]{2,1,0:T(1,128)} %bitcast.14, ...), custom_call_target="tpu_custom_call" | custom-call | tf_op jit(solution)/shard_map/prepare/pallas_call | solution.py:750
  12.6 0.0 copy-done.1
  12.6 0.0 copy-done
  12.6 22.1 %project.1 = (f32[4,4,3,64,8,128]{5,4,3,2,1,0:T(8,128)S(1)}, f32[4,64,8,128]{3,2,1,0:T(8,128)S(1)}, f32[4,6,4,8,128]{4,3,2,1,0:T(8,128)S(1)}) custom-call(bf16[32,2048,128]{2,1,0:T(8,128)(2,1)S(1)} %bitcast.9, bf16[32,256,128]{2,1,0:T(8,128)(2,1)S(1)} %get-tuple-element.14.weights_ref, f32[160,8,128]{2,1,0:T(8,128)S(1)} %bitcast.10, ...), custom_call_target="tpu_custom_call" | custom-call | tf_op jit(solution)/shard_map/project/pallas_call | solution.py:783
  34.7 3.2 %combine.1 = (f32[4,32,64,1,128]{4,3,2,1,0:T(1,128)}, f32[4,32,64,1,128]{4,3,2,1,0:T(1,128)}) custom-call(f32[4,4,3,64,8,128]{5,4,3,2,1,0:T(8,128)S(1)} %get-tuple-element.19.fields_ref, f32[4,64,8,128]{3,2,1,0:T(8,128)S(1)} %get-tuple-element.20.own_ref, f32[4,6,4,8,128]{4,3,2,1,0:T(8,128)S(1)} %get-tuple-element.21.coeff_ref), custom_call_target="tpu_custom_call" | custom-call | tf_op jit(solution)/shard_map/combine/pallas_call | solution.py:817
Async XLA Ops:
  0.6 11.9 %copy-start.1 = (s32[4]{0:T(128)S(1)}, s32[4]{0:T(128)}, u32[]{:S(2)}) copy-start(s32[4]{0:T(128)} %ids_ref.1) | copy-start | bytes 52
  0.6 11.9 %copy-start = (f32[64]{0:T(128)S(1)}, f32[64]{0:T(128)}, u32[]{:S(2)}) copy-start(f32[64]{0:T(128)} %table_ref.1) | copy-start | bytes 772
